TPU v7x, 32 devices: a whole 2x2x4 slice. The times are simulated.
32 devices in a mesh: grid: 8 (over z, y), band: 4 (over x, core).
Axes of the slice: x: 2, y: 2, z: 4, core: 2. Of those that a mesh axis runs over, the one named last changes fastest.
Arguments:
- orbitals: float32 [32, 16, 16, 512], P('grid', None, None, 'band'), may hold values from -80 to 80
- projectors: float32 [32, 16, 16, 512], P('grid', None, None, 'band'), may hold values from -0.09375 to 0.09375
- potential: float32 [32, 16, 16], P('grid'), may hold values from 0.3 to 3
Outputs:
- updated_orbitals: float32 [32, 16, 16, 512], P('grid', None, None, 'band')
- rayleigh_quotients: float32 [3, 512], P(None, 'band')
- residual_norms: float32 [3, 512], P(None, 'band')
All inputs are finite; a program needn't handle non-finite values.
Results may differ from a plain program's by a relative error of at most 0.00012.
Values sent between devices are 32-bit elements; how exact they have to be, the bound alone decides.
A program may use at most 128 MiB of HBM per device.

v0:
```python
import functools

import jax
import jax.numpy as jnp
from jax import lax
from jax.experimental import pallas as pl
from jax.experimental.pallas import tpu as pltpu
from jax.sharding import PartitionSpec as P

ITERS = 3


STENCIL = (-205.0 / 72.0, 8.0 / 5.0, -1.0 / 5.0, 8.0 / 315.0, -1.0 / 560.0)
STEP_LENGTH = 0.25
NORM_EPS = 1e-06
HIGHEST = lax.Precision.HIGHEST
MESH = pl.DeviceIdType.MESH
VMEM = pl.BlockSpec(memory_space=pltpu.VMEM)


def matmul(left, right, precision=HIGHEST):
    return jnp.dot(left, right, precision=precision, preferred_element_type=jnp.float32)


def laplacian(grid_field, low, high):
    padded = jnp.concatenate([low, grid_field, high], axis=0)
    planes_here = grid_field.shape[0]
    result = 3.0 * STENCIL[0] * grid_field
    for distance in range(1, 5):
        result = result + STENCIL[distance] * (
            padded[4 + distance : 4 + distance + planes_here]
            + padded[4 - distance : 4 - distance + planes_here]
        )
    for dimension in (1, 2):
        for distance in range(1, 5):
            result = result + STENCIL[distance] * (
                jnp.roll(grid_field, distance, dimension)
                + jnp.roll(grid_field, -distance, dimension)
            )
    return result


def dot_in_kernel(left, right, contract):
    return lax.dot_general(
        left, right, (contract, ((), ())), precision=HIGHEST, preferred_element_type=jnp.float32
    )


def block_inverse_factor(block):
    size = block.shape[0]
    groups = [block[8 * g : 8 * g + 8, :] for g in range(size // 8)]
    lane = lax.broadcasted_iota(jnp.int32, (8, size), 1)
    sublane = lax.broadcasted_iota(jnp.int32, (8, size), 0)

    def spread_row(value, s):
        return jnp.broadcast_to(value[s : s + 1, :], (8, size))

    def spread_column(value, j):
        return jnp.broadcast_to(value[:, j : j + 1], (8, size))

    finished = []
    for g in range(size // 8):
        first = 8 * g
        inside = (lane >= first) & (lane < first + 8)
        columns = [spread_column(groups[g], first + t) for t in range(8)]
        entry = [[spread_row(columns[t], s) for t in range(s + 1)] for s in range(8)]
        start = jnp.where(inside, jnp.where(lane - first == sublane, 1.0, 0.0), groups[g])
        rows = [spread_row(start, s) for s in range(8)]
        inverse_pivot = []
        factor = [[None] * 8 for _ in range(8)]
        for t in range(8):
            inverse_pivot.append(1.0 / entry[t][t])
            for s in range(t + 1, 8):
                factor[s][t] = entry[s][t] * inverse_pivot[t]
                for u in range(t + 1, s + 1):
                    entry[s][u] = entry[s][u] - factor[s][t] * entry[u][t]
                rows[s] = rows[s] - factor[s][t] * rows[t]
        result = jnp.zeros((8, size), jnp.float32)
        for s in range(8):
            result = jnp.where(sublane == s, rows[s] * (1.0 / jnp.sqrt(entry[s][s])), result)
        finished.append(jnp.where(lane < first + 8, result, 0.0))
        solved = [None] * 8
        for s in reversed(range(8)):
            solved[s] = rows[s] * inverse_pivot[s]
            for t in range(s + 1, 8):
                solved[s] = solved[s] - factor[t][s] * solved[t]
        for i in range(g + 1, size // 8):
            value = jnp.where(inside, 0.0, groups[i])
            for t in range(8):
                value = value - spread_column(groups[i], first + t) * solved[t]
            groups[i] = value
    return jnp.concatenate(finished, axis=0)


def inverse_factor_kernel(size, block, margin_ref, out_ref, work, panel):
    work[...] = margin_ref[...]
    count = size // block

    @pl.loop(0, count)
    def _(k):
        here = pl.ds(pl.multiple_of(k * block, block), block)
        inverse = block_inverse_factor(work[here, here])
        rows = dot_in_kernel(inverse, work[here, :], ((1,), (0,)))
        panel[...] = rows
        work[here, :] = rows
        work[here, here] = inverse

        @pl.loop(k + 1, count)
        def _(i):
            there = pl.ds(pl.multiple_of(i * block, block), block)
            work[there, here] = jnp.zeros((block, block), jnp.float32)
            work[there, :] = work[there, :] - dot_in_kernel(
                panel[:, there], work[here, :], ((0,), (0,))
            )

    for r in range(count):
        rows = pl.ds(r * block, block)
        out_ref[rows, :] = jnp.zeros((block, size), jnp.float32)
        out_ref[rows, : (r + 1) * block] = work[rows, : (r + 1) * block]


def inverse_factor(margin, block):
    size = margin.shape[0]
    return pl.pallas_call(
        functools.partial(inverse_factor_kernel, size, block),
        out_shape=jax.ShapeDtypeStruct((size, size), jnp.float32),
        in_specs=[VMEM],
        out_specs=VMEM,
        scratch_shapes=[
            pltpu.VMEM((size, size), jnp.float32),
            pltpu.VMEM((block, size), jnp.float32),
        ],
    )(margin)


def greet(axis, count, me):
    barrier = pltpu.get_barrier_semaphore()
    for k in range(1, count):
        pl.semaphore_signal(
            barrier, inc=1, device_id={axis: lax.rem(me + k, count)}, device_id_type=MESH
        )
    pl.semaphore_wait(barrier, count - 1)


def remote(axis, peer, source, target, send_sem, recv_sem):
    return pltpu.make_async_remote_copy(
        src_ref=source,
        dst_ref=target,
        send_sem=send_sem,
        recv_sem=recv_sem,
        device_id={axis: peer},
        device_id_type=MESH,
    )


def ring_places(count):
    me = lax.axis_index("band")
    half, side = lax.div(me, 2), lax.rem(me, 2)
    partner = half * 2 + 1 - side
    across = (1 - half) * 2 + side
    return me, partner, across, (1 - half) * 2 + 1 - side


def grid_sum_kernel(count, bands, edge, kind, *refs):
    refs = list(refs)
    x_ref = refs.pop(0)
    extra = refs.pop(0) if kind else None
    out_ref = refs.pop(0)
    extra_out = [refs.pop(0) for _ in range({"": 0, "gather": 1, "halo": 2}[kind])]
    parts, mine, total, s1, r1, s2, r2 = refs[:7]
    me = lax.axis_index("grid")
    chunk = x_ref.shape[0] // count
    barrier = pltpu.get_barrier_semaphore()
    for k in range(1, count):
        pl.semaphore_signal(
            barrier, inc=1, device_id={"grid": lax.rem(me + k, count)}, device_id_type=MESH
        )
    greeted = count - 1
    if kind == "gather":
        place, partner, across, opposite = ring_places(bands)
        for peer in (partner, across):
            pl.semaphore_signal(barrier, inc=1, device_id={"band": peer}, device_id_type=MESH)
        greeted += 2
    pl.semaphore_wait(barrier, greeted)
    if kind == "gather":
        held, send, recv = refs[7:]
        far = remote("band", across, extra, held.at[0], send.at[0], recv.at[0])
        near = remote("band", partner, extra, held.at[1], send.at[1], recv.at[1])
        far.start()
        near.start()
    copies = []
    for k in range(1, count):
        peer = lax.rem(me + k, count)
        copy = remote(
            "grid",
            peer,
            x_ref.at[pl.ds(pl.multiple_of(peer * chunk, chunk), chunk), :],
            parts.at[k - 1],
            s1.at[k - 1],
            r1.at[k - 1],
        )
        copy.start()
        copies.append(copy)
    if kind == "halo":
        held, send, recv = refs[7:]
        cells = extra.shape[0]
        after = remote(
            "grid",
            lax.rem(me + 1, count),
            extra.at[pl.ds(cells - edge, edge), :],
            held.at[0],
            send.at[0],
            recv.at[0],
        )
        before = remote(
            "grid",
            lax.rem(me + count - 1, count),
            extra.at[pl.ds(0, edge), :],
            held.at[1],
            send.at[1],
            recv.at[1],
        )
        after.start()
        before.start()
    own = pl.ds(pl.multiple_of(me * chunk, chunk), chunk)
    mine[...] = x_ref[own, :]
    for k in range(1, count):
        copies[k - 1].wait_recv()
        mine[...] += parts[k - 1]
    total[me] = mine[...]
    back = []
    for k in range(1, count):
        peer = lax.rem(me + k, count)
        copy = remote("grid", peer, mine, total.at[me], s2.at[k - 1], r2.at[k - 1])
        copy.start()
        back.append(copy)
    if kind == "gather":
        width = extra.shape[1]

        def put(source, value):
            extra_out[0][:, pl.ds(pl.multiple_of(source * width, width), width)] = value

        far.wait_recv()
        relay = remote("band", partner, held.at[0], held.at[2], send.at[2], recv.at[2])
        relay.start()
        put(place, extra[...])
        near.wait_recv()
        put(partner, held[1])
        put(across, held[0])
        relay.wait_recv()
        put(opposite, held[2])
        far.wait_send()
        near.wait_send()
        relay.wait_send()
    for k in range(1, count):
        copies[k - 1].wait_send()
        back[k - 1].wait()
    for c in range(count):
        out_ref[c * chunk : (c + 1) * chunk, :] = total[c]
    if kind == "halo":
        after.wait()
        before.wait()
        extra_out[0][...] = held[0]
        extra_out[1][...] = held[1]


def grid_sum(x, collective, kind="", extra=None, edge=0):
    count = lax.axis_size("grid")
    bands = lax.axis_size("band")
    rows, columns = x.shape
    chunk = rows // count
    sems = pltpu.SemaphoreType.DMA((count - 1,))
    out_shape = [jax.ShapeDtypeStruct(x.shape, jnp.float32)]
    more = []
    if kind == "gather":
        cells, width = extra.shape
        out_shape.append(jax.ShapeDtypeStruct((cells, width * bands), jnp.float32))
        more = [pltpu.VMEM((3, cells, width), jnp.float32)]
        more += [pltpu.SemaphoreType.DMA((3,))] * 2
    if kind == "halo":
        width = extra.shape[1]
        out_shape += [jax.ShapeDtypeStruct((edge, width), jnp.float32)] * 2
        more = [pltpu.VMEM((2, edge, width), jnp.float32)]
        more += [pltpu.SemaphoreType.DMA((2,))] * 2
    operands = [x] + ([extra] if kind else [])
    result = pl.pallas_call(
        functools.partial(grid_sum_kernel, count, bands, edge, kind),
        out_shape=out_shape,
        in_specs=[VMEM] * len(operands),
        out_specs=[VMEM] * len(out_shape),
        scratch_shapes=[
            pltpu.VMEM((count - 1, chunk, columns), jnp.float32),
            pltpu.VMEM((chunk, columns), jnp.float32),
            pltpu.VMEM((count, chunk, columns), jnp.float32),
            sems,
            sems,
            sems,
            sems,
        ]
        + more,
        compiler_params=pltpu.CompilerParams(collective_id=collective, has_side_effects=True),
        cost_estimate=pl.CostEstimate(flops=10**6, bytes_accessed=4 * 10**7, transcendentals=0),
    )(*operands)
    return result


def band_gather_kernel(count, x_ref, out_ref, held, send, recv):
    me = lax.axis_index("band")
    width = x_ref.shape[1]
    if count == 4:
        half, side = lax.div(me, 2), lax.rem(me, 2)
        partner = half * 2 + 1 - side
        across = (1 - half) * 2 + side
        barrier = pltpu.get_barrier_semaphore()
        for peer in (partner, across):
            pl.semaphore_signal(barrier, inc=1, device_id={"band": peer}, device_id_type=MESH)
        pl.semaphore_wait(barrier, 2)
        far = remote("band", across, x_ref, held.at[0], send.at[0], recv.at[0])
        far.start()
        near = remote("band", partner, x_ref, held.at[1], send.at[1], recv.at[1])
        near.start()
        out_ref[:, pl.ds(pl.multiple_of(me * width, width), width)] = x_ref[...]
        far.wait_recv()
        relay = remote("band", partner, held.at[0], held.at[2], send.at[2], recv.at[2])
        relay.start()
        near.wait_recv()
        out_ref[:, pl.ds(pl.multiple_of(partner * width, width), width)] = held[1]
        out_ref[:, pl.ds(pl.multiple_of(across * width, width), width)] = held[0]
        relay.wait_recv()
        opposite = (1 - half) * 2 + 1 - side
        out_ref[:, pl.ds(pl.multiple_of(opposite * width, width), width)] = held[2]
        far.wait_send()
        near.wait_send()
        relay.wait_send()
    else:
        greet("band", count, me)
        copies = []
        for k in range(1, count):
            peer = lax.rem(me + k, count)
            copy = remote("band", peer, x_ref, held.at[k - 1], send.at[k - 1], recv.at[k - 1])
            copy.start()
            copies.append(copy)
        out_ref[:, pl.ds(pl.multiple_of(me * width, width), width)] = x_ref[...]
        for k in range(1, count):
            copies[k - 1].wait()
            source = lax.rem(me + count - k, count)
            out_ref[:, pl.ds(pl.multiple_of(source * width, width), width)] = held[k - 1]


def band_gather(x, collective):
    count = lax.axis_size("band")
    rows, columns = x.shape
    return pl.pallas_call(
        functools.partial(band_gather_kernel, count),
        out_shape=jax.ShapeDtypeStruct((rows, columns * count), jnp.float32),
        in_specs=[VMEM],
        out_specs=VMEM,
        scratch_shapes=[
            pltpu.VMEM((count - 1, rows, columns), jnp.float32),
            pltpu.SemaphoreType.DMA((count - 1,)),
            pltpu.SemaphoreType.DMA((count - 1,)),
        ],
        compiler_params=pltpu.CompilerParams(collective_id=collective, has_side_effects=True),
        cost_estimate=pl.CostEstimate(flops=10**6, bytes_accessed=4 * 10**7, transcendentals=0),
    )(x)


def update_kernel(
    count, v_ref, w_ref, out_ref, quotient_ref, norm_ref, part1, part2, all1, all2, s1, r1, s2, r2
):
    me = lax.axis_index("grid")
    cells, bands = v_ref.shape
    greet("grid", count, me)

    def exchange(value, part, everyone, send, recv):
        part[...] = value
        everyone[me] = value
        copies = []
        for k in range(1, count):
            peer = lax.rem(me + k, count)
            copy = remote("grid", peer, part, everyone.at[me], send.at[k - 1], recv.at[k - 1])
            copy.start()
            copies.append(copy)
        for copy in copies:
            copy.wait()
        total = everyone[0]
        for c in range(1, count):
            total = total + everyone[c]
        return jnp.sum(total, axis=0, keepdims=True)

    products = v_ref[...] * w_ref[...]
    quotient = exchange(
        jnp.sum(products.reshape(cells // 8, 8, bands), axis=0), part1, all1, s1, r1
    )
    quotient_ref[...] = quotient
    residual = w_ref[...] - quotient * v_ref[...]
    squared = exchange(
        jnp.sum((residual * residual).reshape(cells // 8, 8, bands), axis=0), part2, all2, s2, r2
    )
    norm_ref[...] = jnp.sqrt(squared)
    factor = STEP_LENGTH / jnp.sqrt(squared + NORM_EPS)
    out_ref[...] = v_ref[...] - (w_ref[...] - quotient * v_ref[...]) * factor


def update(vectors, applied):
    count = lax.axis_size("grid")
    bands = vectors.shape[1]
    sems = pltpu.SemaphoreType.DMA((count - 1,))
    small = pltpu.VMEM((8, bands), jnp.float32)
    everyone = pltpu.VMEM((count, 8, bands), jnp.float32)
    line = jax.ShapeDtypeStruct((1, bands), jnp.float32)
    return pl.pallas_call(
        functools.partial(update_kernel, count),
        out_shape=(jax.ShapeDtypeStruct(vectors.shape, jnp.float32), line, line),
        in_specs=[VMEM, VMEM],
        out_specs=(VMEM, VMEM, VMEM),
        scratch_shapes=[small, small, everyone, everyone, sems, sems, sems, sems],
        compiler_params=pltpu.CompilerParams(collective_id=4, has_side_effects=True),
    )(vectors, applied)


def local(orbitals, projectors, potential):
    grid_shape = orbitals.shape
    local_bands = orbitals.shape[3]
    first_band = lax.axis_index("band") * local_bands
    vectors = orbitals.reshape(-1, local_bands)
    plane = vectors.shape[0] // grid_shape[0]
    projector_rows = projectors.reshape(-1, projectors.shape[3])
    joined = lax.axis_size("band") == 4
    if not joined:
        every_projector = band_gather(projector_rows, 3)
    quotient_list = []
    norm_list = []
    for iteration in range(ITERS):
        gathered = band_gather(vectors, 2)
        share = matmul(gathered.T, vectors)
        if iteration == 0 and joined:
            summed, every_projector = grid_sum(share, 5, "gather", projector_rows)
        else:
            (summed,) = grid_sum(share, 1)
        margin = band_gather(summed, 6)
        inverse = inverse_factor(margin, local_bands)
        rows = lax.dynamic_slice_in_dim(inverse, first_band, local_bands, 0)
        vectors = lax.dot_general(
            gathered,
            rows,
            (((1,), (1,)), ((), ())),
            precision=HIGHEST,
            preferred_element_type=jnp.float32,
        )
        coupling, low, high = grid_sum(
            matmul(every_projector.T, vectors, lax.Precision.HIGH), 7, "halo", vectors, 4 * plane
        )
        exchange_part = matmul(every_projector, coupling, lax.Precision.HIGH)
        grid_field = vectors.reshape(grid_shape)
        applied = (-0.5 * laplacian(
            grid_field, low.reshape(4, *grid_shape[1:]), high.reshape(4, *grid_shape[1:])
        ) + potential[..., None] * grid_field).reshape(
            -1, local_bands
        ) - exchange_part
        vectors, rayleigh, norm = update(vectors, applied)
        quotient_list.append(rayleigh)
        norm_list.append(norm)
    return (
        vectors.reshape(grid_shape),
        jnp.concatenate(quotient_list, axis=0),
        jnp.concatenate(norm_list, axis=0),
    )


def solution(mesh):
    return jax.shard_map(
        local,
        mesh=mesh,
        in_specs=(
            P("grid", None, None, "band"),
            P("grid", None, None, "band"),
            P("grid", None, None),
        ),
        out_specs=(P("grid", None, None, "band"), P(None, "band"), P(None, "band")),
        check_vma=False,
    )
```

profile of v0, /device:TPU:0, one launch (start us, length us, event | category | flops | bytes accessed | tf_op | source)
XLA Modules:
  0.0 478.4 jit_solution(7641901541908655838)
XLA Ops:
  0.6 19.6 %shard_map.58 = f32[1024,512]{1,0:T(8,128)} custom-call(f32[1024,128]{1,0:T(8,128)} %bitcast.91), custom_call_target="tpu_custom_call" | custom-call | flops 1000000 | bytes 40000000 | tf_op jit(solution)/shard_map/pallas_call | solution.py:353
  20.2 5.7 %fusion.147.refs_0_ = f32[512,128]{1,0:T(8,128)} fusion(f32[1024,512]{1,0:T(8,128)} %shard_map.58, f32[1024,128]{1,0:T(8,128)S(1)} %bitcast.92), kind=kOutput, calls=%fused_computation.209 | convolution fusion | flops 805306368 | bytes 2883584 | tf_op jit(solution)/shard_map/dot_general | solution.py:22
  25.9 22.3 %shard_map.59 = (f32[512,128]{1,0:T(8,128)}, f32[1024,512]{1,0:T(8,128)}) custom-call(f32[512,128]{1,0:T(8,128)} %fusion.147.refs_0_, f32[1024,128]{1,0:T(8,128)} %bitcast.102), custom_call_target="tpu_custom_call" | custom-call | flops 1000000 | bytes 40000000 | tf_op jit(solution)/shard_map/pallas_call | solution.py:286
  48.3 11.8 %shard_map.60.margin_ref = f32[512,512]{1,0:T(8,128)} custom-call(f32[512,128]{1,0:T(8,128)} %get-tuple-element.23.x_ref), custom_call_target="tpu_custom_call" | custom-call | flops 1000000 | bytes 40000000 | tf_op jit(solution)/shard_map/pallas_call | solution.py:353
  60.1 31.9 %shard_map.61 = f32[512,512]{1,0:T(8,128)} custom-call(f32[512,512]{1,0:T(8,128)} %shard_map.60.margin_ref), custom_call_target="tpu_custom_call" | custom-call | tf_op jit(solution)/shard_map/pallas_call | solution.py:124
  92.0 3.9 fusion.94
  95.9 2.5 fusion.148.refs_0_
  98.6 0.7 fusion.139
  100.7 0.7 fusion.141
  102.0 0.7 fusion.137
  102.8 0.8 fusion.143
  103.5 0.8 fusion.145
  104.3 1.0 fusion.138
  105.3 0.8 fusion.136
  106.1 1.0 fusion.134
  107.2 0.9 fusion.132
  108.0 34.8 %shard_map.62 = (f32[512,128]{1,0:T(8,128)}, f32[1024,128]{1,0:T(8,128)}, f32[1024,128]{1,0:T(8,128)}) custom-call(f32[512,128]{1,0:T(8,128)} %fusion.148.refs_0_, f32[1024,128]{1,0:T(8,128)} %bitcast.84), custom_call_target="tpu_custom_call" | custom-call | flops 1000000 | bytes 40000000 | tf_op jit(solution)/shard_map/pallas_call | solution.py:286
  142.8 1.3 fusion.144
  146.6 2.7 multiply_add_fusion.2
  149.3 1.8 convolution_subtract_fusion.2.w_ref
  151.1 12.9 %shard_map.63 = (f32[1024,128]{1,0:T(8,128)}, f32[1,128]{1,0:T(1,128)}, f32[1,128]{1,0:T(1,128)}) custom-call(f32[1024,128]{1,0:T(8,128)} %bitcast.86, f32[1024,128]{1,0:T(8,128)} %convolution_subtract_fusion.2.w_ref), custom_call_target="tpu_custom_call" | custom-call | tf_op jit(solution)/shard_map/pallas_call | solution.py:412
  164.0 17.6 %shard_map.64 = f32[1024,512]{1,0:T(8,128)} custom-call(f32[1024,128]{1,0:T(8,128)} %get-tuple-element.28.x_ref), custom_call_target="tpu_custom_call" | custom-call | flops 1000000 | bytes 40000000 | tf_op jit(solution)/shard_map/pallas_call | solution.py:353
  181.6 5.7 %fusion.149.refs_0_ = f32[512,128]{1,0:T(8,128)} fusion(f32[1024,512]{1,0:T(8,128)} %shard_map.64, f32[1024,128]{1,0:T(8,128)S(1)} %copy-done.8), kind=kOutput, calls=%fused_computation.211 | convolution fusion | flops 805306368 | bytes 2883584 | tf_op jit(solution)/shard_map/dot_general | solution.py:22
  187.3 17.3 %shard_map.65.x_ref = f32[512,128]{1,0:T(8,128)} custom-call(f32[512,128]{1,0:T(8,128)} %fusion.149.refs_0_), custom_call_target="tpu_custom_call" | custom-call | flops 1000000 | bytes 40000000 | tf_op jit(solution)/shard_map/pallas_call | solution.py:286
  204.6 11.2 %shard_map.66.margin_ref = f32[512,512]{1,0:T(8,128)} custom-call(f32[512,128]{1,0:T(8,128)} %shard_map.65.x_ref), custom_call_target="tpu_custom_call" | custom-call | flops 1000000 | bytes 40000000 | tf_op jit(solution)/shard_map/pallas_call | solution.py:353
  215.8 31.6 %shard_map.67 = f32[512,512]{1,0:T(8,128)} custom-call(f32[512,512]{1,0:T(8,128)} %shard_map.66.margin_ref), custom_call_target="tpu_custom_call" | custom-call | tf_op jit(solution)/shard_map/pallas_call | solution.py:124
  247.3 3.4 fusion.92.refs_1_.v_ref
  250.7 0.7 fusion.123
  254.1 2.5 fusion.150.refs_0_
  256.7 0.7 fusion.121
  257.4 0.8 fusion.127
  258.1 0.8 fusion.129
  258.9 1.0 fusion.122
  259.9 0.8 fusion.120
  260.8 1.0 fusion.118
  261.8 0.9 fusion.116
  262.6 36.5 %shard_map.68 = (f32[512,128]{1,0:T(8,128)}, f32[1024,128]{1,0:T(8,128)}, f32[1024,128]{1,0:T(8,128)}) custom-call(f32[512,128]{1,0:T(8,128)} %fusion.150.refs_0_, f32[1024,128]{1,0:T(8,128)} %copy-done.2), custom_call_target="tpu_custom_call" | custom-call | flops 1000000 | bytes 40000000 | tf_op jit(solution)/shard_map/pallas_call | solution.py:286
  299.2 1.3 fusion.128
  302.9 2.1 multiply_add_fusion.1
  305.1 1.8 convolution_subtract_fusion.1.w_ref
  306.9 12.6 %shard_map.69 = (f32[1024,128]{1,0:T(8,128)}, f32[1,128]{1,0:T(1,128)}, f32[1,128]{1,0:T(1,128)}) custom-call(f32[1024,128]{1,0:T(8,128)} %copy-done.2, f32[1024,128]{1,0:T(8,128)} %convolution_subtract_fusion.1.w_ref), custom_call_target="tpu_custom_call" | custom-call | tf_op jit(solution)/shard_map/pallas_call | solution.py:412
  319.5 17.6 %shard_map.70 = f32[1024,512]{1,0:T(8,128)} custom-call(f32[1024,128]{1,0:T(8,128)} %get-tuple-element.32.x_ref), custom_call_target="tpu_custom_call" | custom-call | flops 1000000 | bytes 40000000 | tf_op jit(solution)/shard_map/pallas_call | solution.py:353
  337.0 5.7 %fusion.151.refs_0_ = f32[512,128]{1,0:T(8,128)} fusion(f32[1024,512]{1,0:T(8,128)} %shard_map.70, f32[1024,128]{1,0:T(8,128)S(1)} %copy-done.9), kind=kOutput, calls=%fused_computation.213 | convolution fusion | flops 805306368 | bytes 2883584 | tf_op jit(solution)/shard_map/dot_general | solution.py:22
  342.8 17.6 %shard_map.71.x_ref = f32[512,128]{1,0:T(8,128)} custom-call(f32[512,128]{1,0:T(8,128)} %fusion.151.refs_0_), custom_call_target="tpu_custom_call" | custom-call | flops 1000000 | bytes 40000000 | tf_op jit(solution)/shard_map/pallas_call | solution.py:286
  360.4 11.2 %shard_map.72.margin_ref = f32[512,512]{1,0:T(8,128)} custom-call(f32[512,128]{1,0:T(8,128)} %shard_map.71.x_ref), custom_call_target="tpu_custom_call" | custom-call | flops 1000000 | bytes 40000000 | tf_op jit(solution)/shard_map/pallas_call | solution.py:353
  371.6 31.6 %shard_map.73 = f32[512,512]{1,0:T(8,128)} custom-call(f32[512,512]{1,0:T(8,128)} %shard_map.72.margin_ref), custom_call_target="tpu_custom_call" | custom-call | tf_op jit(solution)/shard_map/pallas_call | solution.py:124
  403.2 3.4 fusion.90.refs_1_.v_ref
  406.6 0.7 fusion.107
  408.6 0.7 fusion.109
  410.0 2.5 fusion.152.refs_0_
  412.5 0.7 fusion.105
  413.2 0.8 fusion.111
  414.0 0.8 fusion.113
  414.8 1.0 fusion.106
  415.7 0.8 fusion.104
  416.6 1.0 fusion.102
  417.6 0.9 fusion.100
  418.5 36.8 %shard_map.74 = (f32[512,128]{1,0:T(8,128)}, f32[1024,128]{1,0:T(8,128)}, f32[1024,128]{1,0:T(8,128)}) custom-call(f32[512,128]{1,0:T(8,128)} %fusion.152.refs_0_, f32[1024,128]{1,0:T(8,128)} %copy-done), custom_call_target="tpu_custom_call" | custom-call | flops 1000000 | bytes 40000000 | tf_op jit(solution)/shard_map/pallas_call | solution.py:286
  455.3 1.3 fusion.112
  459.1 2.1 multiply_add_fusion
  461.2 1.8 convolution_subtract_fusion.w_ref
  463.1 11.9 %shard_map.75 = (f32[1024,128]{1,0:T(8,128)}, f32[1,128]{1,0:T(1,128)}, f32[1,128]{1,0:T(1,128)}) custom-call(f32[1024,128]{1,0:T(8,128)} %copy-done, f32[1024,128]{1,0:T(8,128)} %convolution_subtract_fusion.w_ref), custom_call_target="tpu_custom_call" | custom-call | tf_op jit(solution)/shard_map/pallas_call | solution.py:412
  475.0 1.3 pad_maximum_fusion.6
  476.3 1.9 copy.8
  (204 shorter events, 13.4 us)
Async XLA Ops:
  0.6 19.6 %copy-start.7 = (f32[4,16,16,128]{3,2,1,0:T(8,128)S(1)}, f32[4,16,16,128]{3,2,1,0:T(8,128)}, u32[]{:S(2)}) copy-start(f32[4,16,16,128]{3,2,1,0:T(8,128)} %param.3) | copy-start | bytes 1572868
  60.1 35.8 %copy-start.6 = (f32[1024,512]{1,0:T(8,128)S(1)}, f32[1024,512]{1,0:T(8,128)}, u32[]{:S(2)}) copy-start(f32[1024,512]{1,0:T(8,128)} %get-tuple-element.24) | copy-start | bytes 6291460
  98.6 8.5 %copy-start.4 = (f32[128,1024]{0,1:T(8,128)}, f32[128,1024]{0,1:T(8,128)S(1)}, u32[]{:S(2)}) copy-start(f32[128,1024]{0,1:T(8,128)S(1)} %copy.6) | copy-start | bytes 1572868
  108.0 36.1 %copy-start.5 = (f32[128,1024]{0,1:T(8,128)S(1)}, f32[128,1024]{0,1:T(8,128)}, u32[]{:S(2)}) copy-start(f32[128,1024]{0,1:T(8,128)} %copy-done.4) | copy-start | bytes 1572868
  144.3 1.3 copy-start.13
  144.3 1.5 copy-start.14
  144.3 1.6 copy-start.19
  144.3 1.7 copy-start.22
  144.3 1.8 copy-start.23
  144.3 1.8 copy-start.28
  144.4 1.9 copy-start.29
  144.4 1.9 copy-start.34
  144.4 1.9 copy-start.35
  144.4 1.9 copy-start.40
  144.4 2.0 copy-start.41
  144.4 2.1 copy-start.46
  144.4 2.1 copy-start.56
  144.4 2.2 copy-start.57
  144.4 2.1 copy-start.58
  144.4 2.1 copy-start.80
  146.6 2.7 copy-start.74
  164.0 17.6 %copy-start.8 = (f32[1024,128]{1,0:T(8,128)S(1)}, f32[1024,128]{1,0:T(8,128)}, u32[]{:S(2)}) copy-start(f32[1024,128]{1,0:T(8,128)} %get-tuple-element.28.x_ref) | copy-start | bytes 1572868
  250.7 11.1 %copy-start.2 = (f32[1024,128]{1,0:T(8,128)}, f32[1024,128]{1,0:T(8,128)S(1)}, u32[]{:S(2)}) copy-start(f32[1024,128]{1,0:T(8,128)S(1)} %fusion.92.refs_1_.v_ref) | copy-start | bytes 1572868
  262.6 37.8 %copy-start.3 = (f32[1024,128]{1,0:T(8,128)S(1)}, f32[1024,128]{1,0:T(8,128)}, u32[]{:S(2)}) copy-start(f32[1024,128]{1,0:T(8,128)} %copy-done.2) | copy-start | bytes 1572868
  300.6 1.3 copy-start.15
  300.6 1.5 copy-start.16
  300.6 1.6 copy-start.20
  300.6 1.7 copy-start.24
  300.7 1.8 copy-start.25
  300.7 1.8 copy-start.30
  300.7 1.9 copy-start.31
  300.7 1.9 copy-start.36
  300.7 1.9 copy-start.37
  300.7 1.9 copy-start.42
  300.7 2.0 copy-start.43
  300.7 2.1 copy-start.48
  300.7 2.1 copy-start.52
  300.7 2.2 copy-start.53
  300.8 2.1 copy-start.59
  300.8 2.1 copy-start.76
  302.9 2.1 copy-start.75
  319.4 17.6 %copy-start.9 = (f32[1024,128]{1,0:T(8,128)S(1)}, f32[1024,128]{1,0:T(8,128)}, u32[]{:S(2)}) copy-start(f32[1024,128]{1,0:T(8,128)} %get-tuple-element.32.x_ref) | copy-start | bytes 1572868
  406.6 11.1 %copy-start = (f32[1024,128]{1,0:T(8,128)}, f32[1024,128]{1,0:T(8,128)S(1)}, u32[]{:S(2)}) copy-start(f32[1024,128]{1,0:T(8,128)S(1)} %fusion.90.refs_1_.v_ref) | copy-start | bytes 1572868
  418.5 38.1 %copy-start.1 = (f32[1024,128]{1,0:T(8,128)S(1)}, f32[1024,128]{1,0:T(8,128)}, u32[]{:S(2)}) copy-start(f32[1024,128]{1,0:T(8,128)} %copy-done) | copy-start | bytes 1572868
  456.8 1.5 copy-start.18
  456.8 1.6 copy-start.21
  456.8 1.7 copy-start.26
  456.8 1.8 copy-start.27
  456.8 1.8 copy-start.32
  456.8 1.9 copy-start.33
  456.8 1.9 copy-start.38
  456.9 1.9 copy-start.39
  456.9 1.9 copy-start.44
  456.9 2.0 copy-start.45
  456.9 2.1 copy-start.50
  456.9 2.1 copy-start.54
  456.9 2.2 copy-start.55
  456.9 2.1 copy-start.60
  456.9 2.1 copy-start.78
  459.1 2.1 copy-start.73
  461.2 13.7 %copy-start.88 = (f32[1,128]{1,0:T(1,128)S(1)}, f32[1,128]{1,0:T(1,128)}, u32[]{:S(2)}) copy-start(f32[1,128]{1,0:T(1,128)} %get-tuple-element.37) | copy-start | bytes 1540
  461.2 13.7 %copy-start.89 = (f32[1,128]{1,0:T(1,128)S(1)}, f32[1,128]{1,0:T(1,128)}, u32[]{:S(2)}) copy-start(f32[1,128]{1,0:T(1,128)} %get-tuple-element.40) | copy-start | bytes 1540
  461.2 13.7 %copy-start.90 = (f32[1,128]{1,0:T(1,128)S(1)}, f32[1,128]{1,0:T(1,128)}, u32[]{:S(2)}) copy-start(f32[1,128]{1,0:T(1,128)} %get-tuple-element.38) | copy-start | bytes 1540
  461.2 13.7 %copy-start.91 = (f32[1,128]{1,0:T(1,128)S(1)}, f32[1,128]{1,0:T(1,128)}, u32[]{:S(2)}) copy-start(f32[1,128]{1,0:T(1,128)} %get-tuple-element.41) | copy-start | bytes 1540
  (28 other events, 29.5 us)
where the time goes:
time: 483 us; the launch traced here: 478 us
  Pallas kernels  387 us (80%)
  matrix products  40.8 us (8%)
  local copies, waits for them, and re-layouts  40.7 us (8%)
  other arithmetic  8.19 us (2%)
    pallas_call x6, Pallas kernels, grid_sum(): pl.pallas_call(functools.partial(grid_sum_kernel, count, bands, edge, kin...  165 us
    pallas_call x3, Pallas kernels, inverse_factor(): pl.pallas_call(functools.partial(inverse_factor_kernel, size, block), out...  95.1 us
    pallas_call x6, Pallas kernels, band_gather(): pl.pallas_call(functools.partial(band_gather_kernel, count), out_shape=ja...  88.8 us
    pallas_call x3, Pallas kernels, update(): pl.pallas_call(functools.partial(update_kernel, count), out_shape=(jax.Sh...  37.4 us
    slice x48, local copies, waits for them, and re-layouts, laplacian(): jnp.roll(grid_field, distance, dimension)  32.6 us
    dot_general x9, matrix products, matmul(): jnp.dot(left, right, precision=precision, preferred_element_type=jnp.floa...  30.1 us
    dot_general x3, matrix products, local(): lax.dot_general(gathered, rows, (((1,), (1,)), ((), ())), precision=HIGHE...  10.7 us

commit v1 on v0

--- a/solution.py
+++ b/solution.py
@@ -46,26 +46,35 @@
     )
 
 
-def block_inverse_factor(block):
+def block_inverse_factor(block, spread):
     size = block.shape[0]
-    groups = [block[8 * g : 8 * g + 8, :] for g in range(size // 8)]
+    count = size // 8
+    groups = [block[8 * g : 8 * g + 8, :] for g in range(count)]
     lane = lax.broadcasted_iota(jnp.int32, (8, size), 1)
     sublane = lax.broadcasted_iota(jnp.int32, (8, size), 0)
 
-    def spread_row(value, s):
-        return jnp.broadcast_to(value[s : s + 1, :], (8, size))
-
     def spread_column(value, j):
         return jnp.broadcast_to(value[:, j : j + 1], (8, size))
 
     finished = []
-    for g in range(size // 8):
+    for g in range(count):
         first = 8 * g
+        slot = g % 2
         inside = (lane >= first) & (lane < first + 8)
-        columns = [spread_column(groups[g], first + t) for t in range(8)]
-        entry = [[spread_row(columns[t], s) for t in range(s + 1)] for s in range(8)]
+        for t in range(8):
+            spread[slot, 8 * t : 8 * t + 8, :] = spread_column(groups[g], first + t)
         start = jnp.where(inside, jnp.where(lane - first == sublane, 1.0, 0.0), groups[g])
-        rows = [spread_row(start, s) for s in range(8)]
+        spread[slot, 64:72, :] = start
+
+        def stored(at):
+            return jnp.broadcast_to(spread[slot, at : at + 1, :], (8, size))
+
+        entry = [[stored(8 * t + s) for t in range(s + 1)] for s in range(8)]
+        rows = [stored(64 + s) for s in range(8)]
+        following = g + 1 < count
+        if following:
+            ahead = [spread_column(groups[g + 1], first + t) for t in range(8)]
+            value = jnp.where(inside, 0.0, groups[g + 1])
         inverse_pivot = []
         factor = [[None] * 8 for _ in range(8)]
         for t in range(8):
@@ -75,31 +84,38 @@
                 for u in range(t + 1, s + 1):
                     entry[s][u] = entry[s][u] - factor[s][t] * entry[u][t]
                 rows[s] = rows[s] - factor[s][t] * rows[t]
+                if following:
+                    ahead[s] = ahead[s] - factor[s][t] * ahead[t]
+            if following:
+                value = value - (ahead[t] * inverse_pivot[t]) * rows[t]
+        if following:
+            groups[g + 1] = value
         result = jnp.zeros((8, size), jnp.float32)
         for s in range(8):
             result = jnp.where(sublane == s, rows[s] * (1.0 / jnp.sqrt(entry[s][s])), result)
         finished.append(jnp.where(lane < first + 8, result, 0.0))
-        solved = [None] * 8
-        for s in reversed(range(8)):
-            solved[s] = rows[s] * inverse_pivot[s]
-            for t in range(s + 1, 8):
-                solved[s] = solved[s] - factor[t][s] * solved[t]
-        for i in range(g + 1, size // 8):
-            value = jnp.where(inside, 0.0, groups[i])
-            for t in range(8):
-                value = value - spread_column(groups[i], first + t) * solved[t]
-            groups[i] = value
+        if g + 2 < count:
+            solved = [None] * 8
+            for s in reversed(range(8)):
+                solved[s] = rows[s] * inverse_pivot[s]
+                for t in range(s + 1, 8):
+                    solved[s] = solved[s] - factor[t][s] * solved[t]
+            for i in range(g + 2, count):
+                value = jnp.where(inside, 0.0, groups[i])
+                for t in range(8):
+                    value = value - spread_column(groups[i], first + t) * solved[t]
+                groups[i] = value
     return jnp.concatenate(finished, axis=0)
 
 
-def inverse_factor_kernel(size, block, margin_ref, out_ref, work, panel):
+def inverse_factor_kernel(size, block, margin_ref, out_ref, work, panel, spread):
     work[...] = margin_ref[...]
     count = size // block
 
     @pl.loop(0, count)
     def _(k):
         here = pl.ds(pl.multiple_of(k * block, block), block)
-        inverse = block_inverse_factor(work[here, here])
+        inverse = block_inverse_factor(work[here, here], spread)
         rows = dot_in_kernel(inverse, work[here, :], ((1,), (0,)))
         panel[...] = rows
         work[here, :] = rows
@@ -124,12 +140,8 @@
     return pl.pallas_call(
         functools.partial(inverse_factor_kernel, size, block),
         out_shape=jax.ShapeDtypeStruct((size, size), jnp.float32),
-        in_specs=[VMEM],
-        out_specs=VMEM,
-        scratch_shapes=[
-            pltpu.VMEM((size, size), jnp.float32),
-            pltpu.VMEM((block, size), jnp.float32),
-        ],
+        in_specs=[VMEM], out_specs=VMEM,
+        scratch_shapes=[pltpu.VMEM((size, size), jnp.float32), pltpu.VMEM((block, size), jnp.float32), pltpu.VMEM((2,72,block),jnp.float32)],
     )(margin)
 
 

time: 483 us -> 447 us (0.925)
  Pallas kernels: 387 us -> 351 us
    pallas_call x3, Pallas kernels: 95.1 us -> 59.7 us  [inverse_factor(): pl.pallas_call(functools.partial(inverse_factor_kernel, size, block), out...]
where the time goes in v1:
time: 447 us; the launch traced here: 443 us
  Pallas kernels  351 us (79%)
  matrix products  40.8 us (9%)
  local copies, waits for them, and re-layouts  40.7 us (9%)
  other arithmetic  8.19 us (2%)
    pallas_call x6, Pallas kernels, grid_sum(): pl.pallas_call(functools.partial(grid_sum_kernel, count, bands, edge, kin...  165 us
    pallas_call x6, Pallas kernels, band_gather(): pl.pallas_call(functools.partial(band_gather_kernel, count), out_shape=ja...  88.9 us
    pallas_call x3, Pallas kernels, inverse_factor(): pl.pallas_call(functools.partial(inverse_factor_kernel, size, block), out...  59.7 us
    pallas_call x3, Pallas kernels, update(): pl.pallas_call(functools.partial(update_kernel, count), out_shape=(jax.Sh...  37.4 us
    slice x48, local copies, waits for them, and re-layouts, laplacian(): jnp.roll(grid_field, distance, dimension)  32.6 us
    dot_general x9, matrix products, matmul(): jnp.dot(left, right, precision=precision, preferred_element_type=jnp.floa...  30.1 us
    dot_general x3, matrix products, local(): lax.dot_general(gathered, rows, (((1,), (1,)), ((), ())), precision=HIGHE...  10.7 us

profile of v1, /device:TPU:0, one launch (start us, length us, event | category | flops | bytes accessed | tf_op | source)
XLA Modules:
  0.0 443.0 jit_solution(8997946111194922381)
XLA Ops:
  0.6 19.6 %shard_map.58 = f32[1024,512]{1,0:T(8,128)} custom-call(f32[1024,128]{1,0:T(8,128)} %bitcast.91), custom_call_target="tpu_custom_call" | custom-call | flops 1000000 | bytes 40000000 | tf_op jit(solution)/shard_map/pallas_call | solution.py:365
  20.2 5.7 %fusion.147.refs_0_ = f32[512,128]{1,0:T(8,128)} fusion(f32[1024,512]{1,0:T(8,128)} %shard_map.58, f32[1024,128]{1,0:T(8,128)S(1)} %bitcast.92), kind=kOutput, calls=%fused_computation.209 | convolution fusion | flops 805306368 | bytes 2883584 | tf_op jit(solution)/shard_map/dot_general | solution.py:22
  25.9 22.3 %shard_map.59 = (f32[512,128]{1,0:T(8,128)}, f32[1024,512]{1,0:T(8,128)}) custom-call(f32[512,128]{1,0:T(8,128)} %fusion.147.refs_0_, f32[1024,128]{1,0:T(8,128)} %bitcast.102), custom_call_target="tpu_custom_call" | custom-call | flops 1000000 | bytes 40000000 | tf_op jit(solution)/shard_map/pallas_call | solution.py:298
  48.3 11.8 %shard_map.60.margin_ref = f32[512,512]{1,0:T(8,128)} custom-call(f32[512,128]{1,0:T(8,128)} %get-tuple-element.23.x_ref), custom_call_target="tpu_custom_call" | custom-call | flops 1000000 | bytes 40000000 | tf_op jit(solution)/shard_map/pallas_call | solution.py:365
  60.1 20.1 %shard_map.61 = f32[512,512]{1,0:T(8,128)} custom-call(f32[512,512]{1,0:T(8,128)} %shard_map.60.margin_ref), custom_call_target="tpu_custom_call" | custom-call | tf_op jit(solution)/shard_map/pallas_call | solution.py:140
  80.2 3.9 fusion.94
  84.1 2.5 fusion.148.refs_0_
  86.9 0.7 fusion.139
  88.9 0.7 fusion.141
  90.3 0.7 fusion.137
  91.0 0.8 fusion.143
  91.7 0.8 fusion.145
  92.5 1.0 fusion.138
  93.5 0.8 fusion.136
  94.4 1.0 fusion.134
  95.4 0.9 fusion.132
  96.2 34.8 %shard_map.62 = (f32[512,128]{1,0:T(8,128)}, f32[1024,128]{1,0:T(8,128)}, f32[1024,128]{1,0:T(8,128)}) custom-call(f32[512,128]{1,0:T(8,128)} %fusion.148.refs_0_, f32[1024,128]{1,0:T(8,128)} %bitcast.84), custom_call_target="tpu_custom_call" | custom-call | flops 1000000 | bytes 40000000 | tf_op jit(solution)/shard_map/pallas_call | solution.py:298
  131.1 1.3 fusion.144
  134.8 2.7 multiply_add_fusion.2
  137.5 1.8 convolution_subtract_fusion.2.w_ref
  139.3 12.9 %shard_map.63 = (f32[1024,128]{1,0:T(8,128)}, f32[1,128]{1,0:T(1,128)}, f32[1,128]{1,0:T(1,128)}) custom-call(f32[1024,128]{1,0:T(8,128)} %bitcast.86, f32[1024,128]{1,0:T(8,128)} %convolution_subtract_fusion.2.w_ref), custom_call_target="tpu_custom_call" | custom-call | tf_op jit(solution)/shard_map/pallas_call | solution.py:424
  152.2 17.6 %shard_map.64 = f32[1024,512]{1,0:T(8,128)} custom-call(f32[1024,128]{1,0:T(8,128)} %get-tuple-element.28.x_ref), custom_call_target="tpu_custom_call" | custom-call | flops 1000000 | bytes 40000000 | tf_op jit(solution)/shard_map/pallas_call | solution.py:365
  169.8 5.7 %fusion.149.refs_0_ = f32[512,128]{1,0:T(8,128)} fusion(f32[1024,512]{1,0:T(8,128)} %shard_map.64, f32[1024,128]{1,0:T(8,128)S(1)} %copy-done.8), kind=kOutput, calls=%fused_computation.211 | convolution fusion | flops 805306368 | bytes 2883584 | tf_op jit(solution)/shard_map/dot_general | solution.py:22
  175.5 17.3 %shard_map.65.x_ref = f32[512,128]{1,0:T(8,128)} custom-call(f32[512,128]{1,0:T(8,128)} %fusion.149.refs_0_), custom_call_target="tpu_custom_call" | custom-call | flops 1000000 | bytes 40000000 | tf_op jit(solution)/shard_map/pallas_call | solution.py:298
  192.8 11.2 %shard_map.66.margin_ref = f32[512,512]{1,0:T(8,128)} custom-call(f32[512,128]{1,0:T(8,128)} %shard_map.65.x_ref), custom_call_target="tpu_custom_call" | custom-call | flops 1000000 | bytes 40000000 | tf_op jit(solution)/shard_map/pallas_call | solution.py:365
  204.0 19.8 %shard_map.67 = f32[512,512]{1,0:T(8,128)} custom-call(f32[512,512]{1,0:T(8,128)} %shard_map.66.margin_ref), custom_call_target="tpu_custom_call" | custom-call | tf_op jit(solution)/shard_map/pallas_call | solution.py:140
  223.8 3.4 fusion.92.refs_1_.v_ref
  227.2 0.7 fusion.123
  230.6 2.5 fusion.150.refs_0_
  233.1 0.7 fusion.121
  233.8 0.8 fusion.127
  234.6 0.8 fusion.129
  235.3 1.0 fusion.122
  236.3 0.8 fusion.120
  237.2 1.0 fusion.118
  238.2 0.9 fusion.116
  239.1 36.5 %shard_map.68 = (f32[512,128]{1,0:T(8,128)}, f32[1024,128]{1,0:T(8,128)}, f32[1024,128]{1,0:T(8,128)}) custom-call(f32[512,128]{1,0:T(8,128)} %fusion.150.refs_0_, f32[1024,128]{1,0:T(8,128)} %copy-done.2), custom_call_target="tpu_custom_call" | custom-call | flops 1000000 | bytes 40000000 | tf_op jit(solution)/shard_map/pallas_call | solution.py:298
  275.6 1.3 fusion.128
  279.3 2.1 multiply_add_fusion.1
  281.5 1.8 convolution_subtract_fusion.1.w_ref
  283.3 12.6 %shard_map.69 = (f32[1024,128]{1,0:T(8,128)}, f32[1,128]{1,0:T(1,128)}, f32[1,128]{1,0:T(1,128)}) custom-call(f32[1024,128]{1,0:T(8,128)} %copy-done.2, f32[1024,128]{1,0:T(8,128)} %convolution_subtract_fusion.1.w_ref), custom_call_target="tpu_custom_call" | custom-call | tf_op jit(solution)/shard_map/pallas_call | solution.py:424
  295.9 17.6 %shard_map.70 = f32[1024,512]{1,0:T(8,128)} custom-call(f32[1024,128]{1,0:T(8,128)} %get-tuple-element.32.x_ref), custom_call_target="tpu_custom_call" | custom-call | flops 1000000 | bytes 40000000 | tf_op jit(solution)/shard_map/pallas_call | solution.py:365
  313.5 5.7 %fusion.151.refs_0_ = f32[512,128]{1,0:T(8,128)} fusion(f32[1024,512]{1,0:T(8,128)} %shard_map.70, f32[1024,128]{1,0:T(8,128)S(1)} %copy-done.9), kind=kOutput, calls=%fused_computation.213 | convolution fusion | flops 805306368 | bytes 2883584 | tf_op jit(solution)/shard_map/dot_general | solution.py:22
  319.2 17.6 %shard_map.71.x_ref = f32[512,128]{1,0:T(8,128)} custom-call(f32[512,128]{1,0:T(8,128)} %fusion.151.refs_0_), custom_call_target="tpu_custom_call" | custom-call | flops 1000000 | bytes 40000000 | tf_op jit(solution)/shard_map/pallas_call | solution.py:298
  336.8 11.2 %shard_map.72.margin_ref = f32[512,512]{1,0:T(8,128)} custom-call(f32[512,128]{1,0:T(8,128)} %shard_map.71.x_ref), custom_call_target="tpu_custom_call" | custom-call | flops 1000000 | bytes 40000000 | tf_op jit(solution)/shard_map/pallas_call | solution.py:365
  348.0 19.8 %shard_map.73 = f32[512,512]{1,0:T(8,128)} custom-call(f32[512,512]{1,0:T(8,128)} %shard_map.72.margin_ref), custom_call_target="tpu_custom_call" | custom-call | tf_op jit(solution)/shard_map/pallas_call | solution.py:140
  367.8 3.4 fusion.90.refs_1_.v_ref
  371.2 0.7 fusion.107
  373.2 0.7 fusion.109
  374.6 2.5 fusion.152.refs_0_
  377.1 0.7 fusion.105
  377.9 0.8 fusion.111
  378.6 0.8 fusion.113
  379.4 1.0 fusion.106
  380.4 0.8 fusion.104
  381.2 1.0 fusion.102
  382.3 0.9 fusion.100
  383.1 36.8 %shard_map.74 = (f32[512,128]{1,0:T(8,128)}, f32[1024,128]{1,0:T(8,128)}, f32[1024,128]{1,0:T(8,128)}) custom-call(f32[512,128]{1,0:T(8,128)} %fusion.152.refs_0_, f32[1024,128]{1,0:T(8,128)} %copy-done), custom_call_target="tpu_custom_call" | custom-call | flops 1000000 | bytes 40000000 | tf_op jit(solution)/shard_map/pallas_call | solution.py:298
  420.0 1.3 fusion.112
  423.7 2.1 multiply_add_fusion
  425.9 1.8 convolution_subtract_fusion.w_ref
  427.7 11.9 %shard_map.75 = (f32[1024,128]{1,0:T(8,128)}, f32[1,128]{1,0:T(1,128)}, f32[1,128]{1,0:T(1,128)}) custom-call(f32[1024,128]{1,0:T(8,128)} %copy-done, f32[1024,128]{1,0:T(8,128)} %convolution_subtract_fusion.w_ref), custom_call_target="tpu_custom_call" | custom-call | tf_op jit(solution)/shard_map/pallas_call | solution.py:424
  439.6 1.3 pad_maximum_fusion.6
  440.9 1.9 copy.8
  (204 shorter events, 13.4 us)
Async XLA Ops:
  0.6 19.6 %copy-start.7 = (f32[4,16,16,128]{3,2,1,0:T(8,128)S(1)}, f32[4,16,16,128]{3,2,1,0:T(8,128)}, u32[]{:S(2)}) copy-start(f32[4,16,16,128]{3,2,1,0:T(8,128)} %param.3) | copy-start | bytes 1572868
  60.1 24.1 %copy-start.6 = (f32[1024,512]{1,0:T(8,128)S(1)}, f32[1024,512]{1,0:T(8,128)}, u32[]{:S(2)}) copy-start(f32[1024,512]{1,0:T(8,128)} %get-tuple-element.24) | copy-start | bytes 6291460
  86.8 8.5 %copy-start.4 = (f32[128,1024]{0,1:T(8,128)}, f32[128,1024]{0,1:T(8,128)S(1)}, u32[]{:S(2)}) copy-start(f32[128,1024]{0,1:T(8,128)S(1)} %copy.6) | copy-start | bytes 1572868
  96.2 36.1 %copy-start.5 = (f32[128,1024]{0,1:T(8,128)S(1)}, f32[128,1024]{0,1:T(8,128)}, u32[]{:S(2)}) copy-start(f32[128,1024]{0,1:T(8,128)} %copy-done.4) | copy-start | bytes 1572868
  132.5 1.3 copy-start.13
  132.5 1.5 copy-start.14
  132.5 1.6 copy-start.19
  132.5 1.7 copy-start.22
  132.6 1.8 copy-start.23
  132.6 1.8 copy-start.28
  132.6 1.9 copy-start.29
  132.6 1.9 copy-start.34
  132.6 1.9 copy-start.35
  132.6 1.9 copy-start.40
  132.6 2.0 copy-start.41
  132.6 2.1 copy-start.46
  132.6 2.1 copy-start.56
  132.6 2.2 copy-start.57
  132.7 2.1 copy-start.58
  132.7 2.1 copy-start.80
  134.8 2.7 copy-start.74
  152.2 17.6 %copy-start.8 = (f32[1024,128]{1,0:T(8,128)S(1)}, f32[1024,128]{1,0:T(8,128)}, u32[]{:S(2)}) copy-start(f32[1024,128]{1,0:T(8,128)} %get-tuple-element.28.x_ref) | copy-start | bytes 1572868
  227.2 11.1 %copy-start.2 = (f32[1024,128]{1,0:T(8,128)}, f32[1024,128]{1,0:T(8,128)S(1)}, u32[]{:S(2)}) copy-start(f32[1024,128]{1,0:T(8,128)S(1)} %fusion.92.refs_1_.v_ref) | copy-start | bytes 1572868
  239.1 37.8 %copy-start.3 = (f32[1024,128]{1,0:T(8,128)S(1)}, f32[1024,128]{1,0:T(8,128)}, u32[]{:S(2)}) copy-start(f32[1024,128]{1,0:T(8,128)} %copy-done.2) | copy-start | bytes 1572868
  277.1 1.3 copy-start.15
  277.1 1.5 copy-start.16
  277.1 1.6 copy-start.20
  277.1 1.7 copy-start.24
  277.1 1.8 copy-start.25
  277.1 1.8 copy-start.30
  277.1 1.9 copy-start.31
  277.1 1.9 copy-start.36
  277.1 1.9 copy-start.37
  277.1 1.9 copy-start.42
  277.2 2.0 copy-start.43
  277.2 2.1 copy-start.48
  277.2 2.1 copy-start.52
  277.2 2.2 copy-start.53
  277.2 2.1 copy-start.59
  277.2 2.1 copy-start.76
  279.3 2.1 copy-start.75
  295.9 17.6 %copy-start.9 = (f32[1024,128]{1,0:T(8,128)S(1)}, f32[1024,128]{1,0:T(8,128)}, u32[]{:S(2)}) copy-start(f32[1024,128]{1,0:T(8,128)} %get-tuple-element.32.x_ref) | copy-start | bytes 1572868
  371.2 11.1 %copy-start = (f32[1024,128]{1,0:T(8,128)}, f32[1024,128]{1,0:T(8,128)S(1)}, u32[]{:S(2)}) copy-start(f32[1024,128]{1,0:T(8,128)S(1)} %fusion.90.refs_1_.v_ref) | copy-start | bytes 1572868
  383.1 38.1 %copy-start.1 = (f32[1024,128]{1,0:T(8,128)S(1)}, f32[1024,128]{1,0:T(8,128)}, u32[]{:S(2)}) copy-start(f32[1024,128]{1,0:T(8,128)} %copy-done) | copy-start | bytes 1572868
  421.4 1.5 copy-start.18
  421.4 1.6 copy-start.21
  421.4 1.7 copy-start.26
  421.5 1.8 copy-start.27
  421.5 1.8 copy-start.32
  421.5 1.9 copy-start.33
  421.5 1.9 copy-start.38
  421.5 1.9 copy-start.39
  421.5 1.9 copy-start.44
  421.5 2.0 copy-start.45
  421.5 2.1 copy-start.50
  421.5 2.1 copy-start.54
  421.5 2.2 copy-start.55
  421.6 2.1 copy-start.60
  421.6 2.1 copy-start.78
  423.7 2.1 copy-start.73
  425.9 13.8 %copy-start.88 = (f32[1,128]{1,0:T(1,128)S(1)}, f32[1,128]{1,0:T(1,128)}, u32[]{:S(2)}) copy-start(f32[1,128]{1,0:T(1,128)} %get-tuple-element.37) | copy-start | bytes 1540
  425.9 13.8 %copy-start.89 = (f32[1,128]{1,0:T(1,128)S(1)}, f32[1,128]{1,0:T(1,128)}, u32[]{:S(2)}) copy-start(f32[1,128]{1,0:T(1,128)} %get-tuple-element.40) | copy-start | bytes 1540
  425.9 13.8 %copy-start.90 = (f32[1,128]{1,0:T(1,128)S(1)}, f32[1,128]{1,0:T(1,128)}, u32[]{:S(2)}) copy-start(f32[1,128]{1,0:T(1,128)} %get-tuple-element.38) | copy-start | bytes 1540
  425.9 13.8 %copy-start.91 = (f32[1,128]{1,0:T(1,128)S(1)}, f32[1,128]{1,0:T(1,128)}, u32[]{:S(2)}) copy-start(f32[1,128]{1,0:T(1,128)} %get-tuple-element.41) | copy-start | bytes 1540
  (28 other events, 29.5 us)

commit v2 on v1

v2 whole, which is shorter than its diff:
```python
import functools

import jax
import jax.numpy as jnp
from jax import lax
from jax.experimental import pallas as pl
from jax.experimental.pallas import tpu as pltpu
from jax.sharding import PartitionSpec as P

ITERS = 3


STENCIL = (-205.0 / 72.0, 8.0 / 5.0, -1.0 / 5.0, 8.0 / 315.0, -1.0 / 560.0)
STEP_LENGTH = 0.25
NORM_EPS = 1e-06
HIGHEST = lax.Precision.HIGHEST
MESH = pl.DeviceIdType.MESH
VMEM = pl.BlockSpec(memory_space=pltpu.VMEM)
PIECES = 4
WIDE = 256
BF16 = jnp.bfloat16
F32 = jnp.float32


def exact_dot(left, right, contract):
    return lax.dot_general(
        left, right, (contract, ((), ())), precision=HIGHEST, preferred_element_type=F32
    )


def plain_dot(left, right, contract):
    return lax.dot_general(left, right, (contract, ((), ())), preferred_element_type=F32)


def split(value, parts):
    pieces = []
    for _ in range(parts - 1):
        head = value.astype(BF16)
        pieces.append(head)
        value = value - head.astype(F32)
    pieces.append(value.astype(BF16))
    return pieces


def split_dot(left, right, contract):
    total = None
    for order in reversed(range(max(len(left), len(right)))):
        for i in range(order + 1):
            if i < len(left) and order - i < len(right):
                term = plain_dot(left[i], right[order - i], contract)
                total = term if total is None else total + term
    return total


def block_inverse_factor(block, spread):
    size = block.shape[0]
    count = size // 8
    groups = [block[8 * g : 8 * g + 8, :] for g in range(count)]
    lane = lax.broadcasted_iota(jnp.int32, (8, size), 1)
    sublane = lax.broadcasted_iota(jnp.int32, (8, size), 0)

    def spread_column(value, j):
        return jnp.broadcast_to(value[:, j : j + 1], (8, size))

    finished = []
    for g in range(count):
        first = 8 * g
        slot = g % 2
        inside = (lane >= first) & (lane < first + 8)
        for t in range(8):
            spread[slot, 8 * t : 8 * t + 8, :] = spread_column(groups[g], first + t)
        start = jnp.where(inside, jnp.where(lane - first == sublane, 1.0, 0.0), groups[g])
        spread[slot, 64:72, :] = start

        def stored(at):
            return jnp.broadcast_to(spread[slot, at : at + 1, :], (8, size))

        entry = [[stored(8 * t + s) for t in range(s + 1)] for s in range(8)]
        rows = [stored(64 + s) for s in range(8)]
        following = g + 1 < count
        if following:
            ahead = [spread_column(groups[g + 1], first + t) for t in range(8)]
            value = jnp.where(inside, 0.0, groups[g + 1])
        inverse_pivot = []
        factor = [[None] * 8 for _ in range(8)]
        for t in range(8):
            inverse_pivot.append(1.0 / entry[t][t])
            for s in range(t + 1, 8):
                factor[s][t] = entry[s][t] * inverse_pivot[t]
                for u in range(t + 1, s + 1):
                    entry[s][u] = entry[s][u] - factor[s][t] * entry[u][t]
                rows[s] = rows[s] - factor[s][t] * rows[t]
                if following:
                    ahead[s] = ahead[s] - factor[s][t] * ahead[t]
            if following:
                value = value - (ahead[t] * inverse_pivot[t]) * rows[t]
        if following:
            groups[g + 1] = value
        result = jnp.zeros((8, size), F32)
        for s in range(8):
            result = jnp.where(sublane == s, rows[s] * (1.0 / jnp.sqrt(entry[s][s])), result)
        finished.append(jnp.where(lane < first + 8, result, 0.0))
        if g + 2 < count:
            solved = [None] * 8
            for s in reversed(range(8)):
                solved[s] = rows[s] * inverse_pivot[s]
                for t in range(s + 1, 8):
                    solved[s] = solved[s] - factor[t][s] * solved[t]
            for i in range(g + 2, count):
                value = jnp.where(inside, 0.0, groups[i])
                for t in range(8):
                    value = value - spread_column(groups[i], first + t) * solved[t]
                groups[i] = value
    return jnp.concatenate(finished, axis=0)


def remote(axis, peer, source, target, send_sem, recv_sem):
    return pltpu.make_async_remote_copy(
        src_ref=source,
        dst_ref=target,
        send_sem=send_sem,
        recv_sem=recv_sem,
        device_id={axis: peer},
        device_id_type=MESH,
    )


class BandGather:
    def __init__(self, source, target, place, sems):
        send, recv = sems
        me, partner, across = place
        self.copies = []
        rows = target.shape[2] // PIECES
        for q in range(PIECES):
            part = pl.ds(q * rows, rows)

            def block(owner, part=part):
                return target.at[owner, :, part, :]

            here = source.at[:, part, :]
            far = remote("band", across, here, block(me), send.at[0, q], recv.at[0, q])
            near = remote("band", partner, here, block(me), send.at[1, q], recv.at[1, q])
            relay = remote(
                "band", partner, block(across), block(across), send.at[2, q], recv.at[2, q]
            )
            self.copies.append((far, near, relay))

    def start(self):
        for far, _, _ in self.copies:
            far.start()
        for _, near, _ in self.copies:
            near.start()

    def pass_on(self):
        for far, _, relay in self.copies:
            far.wait_recv()
            relay.start()

    def finish(self):
        for far, near, relay in self.copies:
            near.wait_recv()
            relay.wait_recv()
        for far, near, relay in self.copies:
            far.wait_send()
            near.wait_send()
            relay.wait_send()


class GridSum:
    def __init__(self, part, arrived, mine, target, me, count, sems):
        s1, r1, s2, r2 = sems
        self.part, self.arrived, self.mine, self.target = part, arrived, mine, target
        chunk = mine.shape[0]
        self.own = pl.ds(pl.multiple_of(me * chunk, chunk), chunk)
        self.out, self.back = [], []
        for k in range(1, count):
            peer = lax.rem(me + k, count)
            there = pl.ds(pl.multiple_of(peer * chunk, chunk), chunk)
            self.out.append(
                remote("grid", peer, part.at[there, :], arrived.at[k - 1], s1.at[k - 1], r1.at[k - 1])
            )
            self.back.append(
                remote("grid", peer, mine, target.at[self.own, :], s2.at[k - 1], r2.at[k - 1])
            )

    def scatter(self):
        for copy in self.out:
            copy.start()

    def add(self):
        total = self.part[self.own, :]
        for k, copy in enumerate(self.out):
            copy.wait_recv()
            total = total + self.arrived[k]
        self.mine[...] = total
        for copy in self.back:
            copy.start()
        self.target[self.own, :] = total

    def finish(self):
        for copy in self.back:
            copy.wait_recv()
        for copy in self.out + self.back:
            copy.wait_send()


def iterations_kernel(count, bands, ny, *refs):
    (u0, x0, pot, out_ref, quot_ref, norm_ref) = refs[:6]
    (
        u, xr, kk, wb, uh, um, ul, xh, xm, kh, km, lh, lm, ll, work, panel, spread,
        spart, cpart, sin, cin, smine, cmine, csum, sall, hz, hs, hr, stat, stats, lam,
        sums_s, sums_c, gat_u, gat_x, gat_s, gat_k, halo_z, halo_y, stat_s, stat_r,
    ) = refs[6:]
    me = lax.axis_index("grid")
    band = lax.axis_index("band")
    half, side = lax.div(band, 2), lax.rem(band, 2)
    partner = half * 2 + 1 - side
    across = (1 - half) * 2 + side
    place = (band, partner, across)
    planes, plane, w = u0.shape
    n = planes * plane
    total = bands * w
    nx = plane // ny

    barrier = pltpu.get_barrier_semaphore()
    for k in range(1, count):
        pl.semaphore_signal(
            barrier, inc=1, device_id={"grid": lax.rem(me + k, count)}, device_id_type=MESH
        )
    for peer in (partner, across):
        pl.semaphore_signal(barrier, inc=1, device_id={"band": peer}, device_id_type=MESH)
    pl.semaphore_wait(barrier, count + 1)

    stat[...] = jnp.zeros_like(stat)
    gather_u = BandGather(u0, u, place, (gat_u.at[0], gat_u.at[1]))
    gather_x = BandGather(x0, xr, place, (gat_x.at[0], gat_x.at[1]))
    gather_u.start()
    gather_x.start()
    u[band] = u0[...]
    xr[band] = x0[...]
    gather_u.pass_on()
    gather_u.finish()

    odd = lax.rem(me, 2)
    z_peer = lax.rem(me + count + 4 * odd - 2, count)
    y_peer = me + 1 - 2 * odd
    part_rows = plane // PIECES

    def lanes(j):
        return slice(j * w, (j + 1) * w)

    def split_blocks(source, targets):
        for j in range(bands):
            @pl.loop(0, planes)
            def _(p):
                rows = pl.ds(pl.multiple_of(p * plane, plane), plane)
                for target, piece in zip(targets, split(source[j, p], len(targets))):
                    target[rows, lanes(j)] = piece

    def iteration(it):
        sum_s = GridSum(spart, sin, smine, sall.at[band], me, count, [sums_s.at[i] for i in range(4)])
        sum_c = GridSum(cpart, cin, cmine, csum, me, count, [sums_c.at[i] for i in range(4)])
        gather_s = BandGather(
            sall.at[band].reshape(1, total, w), sall.reshape(bands, 1, total, w), place,
            (gat_s.at[0], gat_s.at[1]),
        )
        gather_k = BandGather(kk.at[band], kk, place, (gat_k.at[0], gat_k.at[1]))
        across_z, across_y = [], []
        for q in range(PIECES):
            part = pl.ds(q * part_rows, part_rows)
            across_z.append(
                remote("grid", z_peer, u.at[band, :, part, :], hz.at[:, part, :],
                       halo_z.at[0, q], halo_z.at[1, q])
            )
            across_y.append(
                remote("grid", y_peer, hs.at[:, part, :], hr.at[:, part, :],
                       halo_y.at[0, q], halo_y.at[1, q])
            )

        across_z[0].start()
        split_blocks(u, (uh, um, ul))
        turned = split(jnp.transpose(u[band].reshape(n, w)), 3)
        for start in range(0, total, WIDE):
            wide = slice(start, start + WIDE)
            tile = split_dot(turned, [uh[:, wide], um[:, wide], ul[:, wide]], ((1,), (0,)))
            for c in range(WIDE // w):
                at = start + c * w
                spart[at : at + w, :] = tile[:, lanes(c)]
        sum_s.scatter()
        across_z[1].start()

        @pl.when(it == 0)
        def _():
            gather_x.pass_on()
            gather_x.finish()
            split_blocks(xr, (xh, xm))

        for start in range(0, total, WIDE):
            wide = slice(start, start + WIDE)
            tile = split_dot(turned[:2], [xh[:, wide], xm[:, wide]], ((1,), (0,)))
            for c in range(WIDE // w):
                at = start + c * w
                cpart[at : at + w, :] = tile[:, lanes(c)]

        def halo_part(q):
            across_z[q].wait_recv()
            for own_above in (0, 1):
                @pl.when(odd == own_above)
                def _():
                    @pl.loop(0, part_rows // 16)
                    def _(r):
                        rows = pl.ds(pl.multiple_of(q * part_rows + r * 16, 16), 16)
                        own = [u[band, j, rows, :] for j in range(planes)]
                        other = [hz[j, rows, :] for j in range(planes)]
                        below, above = (other, own) if own_above else (own, other)
                        for p in range(planes):
                            value = None
                            for d in range(1, 5):
                                terms = []
                                if p - d < 0:
                                    terms.append(below[planes + p - d])
                                if p + d >= planes:
                                    terms.append(above[p + d - planes])
                                for term in terms:
                                    term = STENCIL[d] * term
                                    value = term if value is None else value + term
                            hs[p, rows, :] = value
            across_y[q].start()

        sum_s.add()
        sum_c.scatter()
        across_z[2].start()
        across_z[3].start()
        halo_part(0)
        halo_part(1)

        @pl.loop(0, nx)
        def _(x):
            def rows_at(at):
                return pl.ds(pl.multiple_of(lax.rem(at + nx, nx) * ny, ny), ny)

            rows = rows_at(x)
            field = [u[band, p, rows, :] for p in range(planes)]
            for p in range(planes):
                value = 3.0 * STENCIL[0] * field[p]
                for d in range(1, 5):
                    near = u[band, p, rows_at(x + d), :] + u[band, p, rows_at(x - d), :]
                    near = near + pltpu.roll(field[p], d, 0) + pltpu.roll(field[p], ny - d, 0)
                    if p - d >= 0:
                        near = near + field[p - d]
                    if p + d < planes:
                        near = near + field[p + d]
                    value = value + STENCIL[d] * near
                kk[band, p, rows, :] = -0.5 * value + pot[p, rows, :] * field[p]

        sum_s.finish()
        gather_s.start()
        halo_part(2)
        halo_part(3)
        sum_c.add()
        gather_s.pass_on()
        gather_s.finish()
        for b in range(bands):
            for c in range(bands):
                work[b * w : (b + 1) * w, lanes(c)] = sall[b, c * w : (c + 1) * w, :]

        def exchange_and_send():
            sum_c.finish()
            coupling = jnp.concatenate(
                [jnp.transpose(csum[c * w : (c + 1) * w, :]) for c in range(bands)], axis=0
            )
            right = split(coupling, 2)
            for copy in across_y:
                copy.wait_recv()

            @pl.loop(0, planes)
            def _(p):
                rows = pl.ds(pl.multiple_of(p * plane, plane), plane)
                exchange = split_dot([xh[rows, :], xm[rows, :]], right, ((1,), (0,)))
                kk[band, p] = kk[band, p] - 0.5 * hr[p] - exchange
            gather_k.start()

        @pl.loop(0, bands)
        def _(k):
            here = pl.ds(pl.multiple_of(k * w, w), w)
            inverse = block_inverse_factor(work[here, here], spread)
            rows = exact_dot(inverse, work[here, :], ((1,), (0,)))
            panel[...] = rows
            work[here, :] = rows
            work[here, here] = inverse

            @pl.loop(k + 1, bands)
            def _(i):
                there = pl.ds(pl.multiple_of(i * w, w), w)
                work[there, here] = jnp.zeros((w, w), F32)
                work[there, :] = work[there, :] - exact_dot(
                    panel[:, there], work[here, :], ((0,), (0,))
                )

            @pl.when(k == 1)
            def _():
                exchange_and_send()

        gather_k.pass_on()
        for r in range(bands):
            rows = slice(r * w, (r + 1) * w)
            for target, piece in zip((lh, lm, ll), split(work[rows, :], 3)):
                target[rows, : (r + 1) * w] = piece[:, : (r + 1) * w]
                if (r + 1) * w < total:
                    target[rows, (r + 1) * w :] = jnp.zeros((w, total - (r + 1) * w), BF16)
        gather_k.finish()
        split_blocks(kk, (kh, km))
        for copy in across_z + across_y:
            copy.wait_send()

        @pl.loop(0, planes)
        def _(p):
            rows = pl.ds(pl.multiple_of(p * plane, plane), plane)
            for start in range(0, total, WIDE):
                deep = slice(0, start + WIDE)
                wide = slice(start, start + WIDE)
                right = [lh[wide, deep], lm[wide, deep], ll[wide, deep]]
                v = split_dot([uh[rows, deep], um[rows, deep], ul[rows, deep]], right, ((1,), (1,)))
                t = split_dot([kh[rows, deep], km[rows, deep]], right[:2], ((1,), (1,)))
                for c in range(WIDE // w):
                    u[start // w + c, p] = v[:, lanes(c)]
                    wb[start // w + c, p] = t[:, lanes(c)]

        def column_sum(value):
            return jnp.sum(value, axis=0, keepdims=True)

        def eight(value):
            return jnp.sum(value.reshape(plane // 8, 8, w), axis=0)

        for j in range(bands):
            zero = jnp.zeros((8, w), F32)

            def first(p, carry, j=j):
                v, t = u[j, p], wb[j, p]
                return carry[0] + eight(v * t), carry[1] + eight(v * v)

            vw, vv = lax.fori_loop(0, planes, first, (zero, zero))
            vw, vv = column_sum(vw), column_sum(vv)
            slope = jnp.where(vv > 1e-12, vw / jnp.maximum(vv, 1e-12), 0.0)

            def second(p, carry, j=j, slope=slope):
                r = wb[j, p] - slope * u[j, p]
                return carry + eight(r * r)

            rest = column_sum(lax.fori_loop(0, planes, second, zero))
            stat[j : j + 1, :] = vw
            stat[bands + j : bands + j + 1, :] = vv
            stat[2 * bands + j : 2 * bands + j + 1, :] = rest

        copies = []
        for k in range(1, count):
            peer = lax.rem(me + k, count)
            copy = remote("grid", peer, stat, stats.at[me], stat_s.at[k - 1], stat_r.at[k - 1])
            copy.start()
            copies.append(copy)
        stats[me] = stat[...]
        for copy in copies:
            copy.wait()
        quotient = stats[0, :bands, :]
        for c in range(1, count):
            quotient = quotient + stats[c, :bands, :]
        squared = jnp.zeros((bands, w), F32)
        for c in range(count):
            vw, vv = stats[c, :bands, :], stats[c, bands : 2 * bands, :]
            slope = jnp.where(vv > 1e-12, vw / jnp.maximum(vv, 1e-12), 0.0)
            shift = slope - quotient
            squared = squared + stats[c, 2 * bands : 3 * bands, :]
            squared = squared + shift * (2.0 * (vw - slope * vv) + shift * vv)
        squared = jnp.maximum(squared, 0.0)
        lam[0, :bands, :] = quotient
        lam[1, :bands, :] = jnp.sqrt(squared)
        lam[2, :bands, :] = STEP_LENGTH / jnp.sqrt(squared + NORM_EPS)
        quot_ref[pl.ds(it, 1), :] = lam[0, pl.ds(band, 1), :]
        norm_ref[pl.ds(it, 1), :] = lam[1, pl.ds(band, 1), :]
        for j in range(bands):
            rate, length = lam[0, j : j + 1, :], lam[2, j : j + 1, :]

            @pl.loop(0, planes)
            def _(p, j=j, rate=rate, length=length):
                v = u[j, p]
                u[j, p] = v - (wb[j, p] - rate * v) * length

    @pl.loop(0, ITERS)
    def _(it):
        iteration(it)

    out_ref[...] = u[band]


def local(orbitals, projectors, potential):
    grid_shape = orbitals.shape
    planes, nx, ny, w = grid_shape
    plane = nx * ny
    n = planes * plane
    count = lax.axis_size("grid")
    bands = lax.axis_size("band")
    total = bands * w
    chunk = total // count
    field = (planes, plane, w)
    block = pltpu.VMEM((bands,) + field, F32)
    half = pltpu.VMEM((n, total), BF16)
    square = pltpu.VMEM((total, total), BF16)
    column = pltpu.VMEM((total, w), F32)
    arrived = pltpu.VMEM((count - 1, chunk, w), F32)
    mine = pltpu.VMEM((chunk, w), F32)
    slab = pltpu.VMEM(field, F32)
    dma = pltpu.SemaphoreType.DMA
    spread_potential = jnp.broadcast_to(potential.reshape(planes, plane, 1), field)
    line = jax.ShapeDtypeStruct((ITERS, w), F32)
    updated, quotients, norms = pl.pallas_call(
        functools.partial(iterations_kernel, count, bands, ny),
        out_shape=(jax.ShapeDtypeStruct(field, F32), line, line),
        in_specs=[VMEM] * 3,
        out_specs=(VMEM, VMEM, VMEM),
        scratch_shapes=[block] * 4
        + [half] * 7
        + [square] * 3
        + [
            pltpu.VMEM((total, total), F32),
            pltpu.VMEM((w, total), F32),
            pltpu.VMEM((2, 72, w), F32),
        ]
        + [column, column, arrived, arrived, mine, mine, column]
        + [pltpu.VMEM((bands, total, w), F32), slab, slab, slab]
        + [
            pltpu.VMEM((16, w), F32),
            pltpu.VMEM((count, 16, w), F32),
            pltpu.VMEM((3, 8, w), F32),
        ]
        + [dma((4, count - 1))] * 2
        + [dma((2, 3, PIECES))] * 4
        + [dma((2, PIECES))] * 2
        + [dma((count - 1,))] * 2,
        compiler_params=pltpu.CompilerParams(
            collective_id=0, has_side_effects=True, vmem_limit_bytes=60 * 2**20
        ),
    )(orbitals.reshape(field), projectors.reshape(field), spread_potential)
    return updated.reshape(grid_shape), quotients, norms


def solution(mesh):
    return jax.shard_map(
        local,
        mesh=mesh,
        in_specs=(
            P("grid", None, None, "band"),
            P("grid", None, None, "band"),
            P("grid", None, None),
        ),
        out_specs=(P("grid", None, None, "band"), P(None, "band"), P(None, "band")),
        check_vma=False,
    )
```

time: 447 us -> 249 us (0.56)
  Pallas kernels: 351 us -> 243 us
  matrix products: 40.8 us -> 0 us
  local copies, waits for them, and re-layouts: 40.7 us -> 4.97 us
  other arithmetic: 8.19 us -> 0 us
    pallas_call x18 -> x1, Pallas kernels: 351 us -> 243 us  [local(): pl.pallas_call(functools.partial(iterations_kernel, count, bands, ny), ou...]
    dot_general x12 -> x0, matrix products: 40.8 us -> none  [the longest x9 30.1 us: matmul(): jnp.dot(left, right, precision=precision, preferred_element_type=jnp.floa...]
    slice x48 -> x0, local copies, waits for them, and re-layouts: 32.6 us -> none  [laplacian(): jnp.roll(grid_field, distance, dimension)]
    add x3 -> x0, other arithmetic: 6.92 us -> none  [local(): -0.5]
    unnamed x185 -> x7, local copies, waits for them, and re-layouts: 7.91 us -> 3.14 us
where the time goes in v2:
time: 249 us
  Pallas kernels  243 us (98%)
  local copies, waits for them, and re-layouts  4.97 us (2%)
    pallas_call x1, Pallas kernels, local(): pl.pallas_call(functools.partial(iterations_kernel, count, bands, ny), ou...  243 us

profile of v2, /device:TPU:0, one launch (start us, length us, event | category | flops | bytes accessed | tf_op | source)
XLA Modules:
  0.0 248.8 jit_solution(1988302770781118171)
XLA Ops:
  0.6 0.8 broadcast_in_dim.7
  1.5 1.0 broadcast_in_dim.8.refs_2_
  2.5 243.2 %shard_map.58 = (f32[4,256,128]{2,1,0:T(8,128)}, f32[3,128]{1,0:T(4,128)}, f32[3,128]{1,0:T(4,128)}) custom-call(f32[4,256,128]{2,1,0:T(8,128)} %bitcast.3, f32[4,256,128]{2,1,0:T(8,128)} %bitcast.4, f32[4,256,128]{2,1,0:T(8,128)} %broadcast_in_dim.8.refs_2_), custom_call_target="tpu_custom_call" | custom-call | tf_op jit(solution)/shard_map/pallas_call | solution.py:515
  245.7 0.0 copy-start.1
  245.7 1.9 copy.9
  247.6 0.0 copy-done.1
  247.6 0.0 copy-start
  247.6 0.6 copy.10
  248.1 0.1 copy-done
  248.2 0.6 copy.11
Async XLA Ops:
  245.7 1.9 copy-start.1
  247.6 0.7 copy-start

commit v3 on v2

--- a/solution.py
+++ b/solution.py
@@ -151,8 +151,8 @@
         for _, near, _ in self.copies:
             near.start()
 
-    def pass_on(self):
-        for far, _, relay in self.copies:
+    def pass_on(self, first=0, last=PIECES):
+        for far, _, relay in self.copies[first:last]:
             far.wait_recv()
             relay.start()
 
@@ -166,41 +166,89 @@
             relay.wait_send()
 
 
+def far_first(me, count):
+    low = 2 * me < count
+    peers = []
+    for k in range(count - 1):
+        down = count - 1 - k
+        down = jnp.where(down > me, down, down - 1)
+        up = jnp.where(k < me, k, k + 1)
+        peers.append(jnp.where(low, down, up))
+    return peers
+
+
 class GridSum:
-    def __init__(self, part, arrived, mine, target, me, count, sems):
-        s1, r1, s2, r2 = sems
-        self.part, self.arrived, self.mine, self.target = part, arrived, mine, target
-        chunk = mine.shape[0]
-        self.own = pl.ds(pl.multiple_of(me * chunk, chunk), chunk)
-        self.out, self.back = [], []
-        for k in range(1, count):
-            peer = lax.rem(me + k, count)
-            there = pl.ds(pl.multiple_of(peer * chunk, chunk), chunk)
-            self.out.append(
-                remote("grid", peer, part.at[there, :], arrived.at[k - 1], s1.at[k - 1], r1.at[k - 1])
+    def __init__(self, part, paired, arrived, middle, target, me, count, sems):
+        pair_s, pair_r, far_s, far_r, back_s, back_r, pass_s, pass_r = sems
+        self.part, self.paired, self.arrived, self.held, self.target = (
+            part, paired, arrived, middle, target,
+        )
+        chunk = middle.shape[1]
+        half = count // 2
+        place, side = lax.div(me, 2), lax.rem(me, 2)
+        pair = me + 1 - 2 * side
+        self.order = far_first(place, half) + [place]
+        self.last = half - 1
+
+        def rows(parity, owner):
+            return pl.ds(pl.multiple_of((parity * half + owner) * chunk, chunk), chunk)
+
+        self.mine = [rows(side, owner) for owner in self.order]
+        self.pairs, self.far, self.far_in, self.back, self.back_in, self.passed = [], [], [], [], [], []
+        own = middle.at[self.last]
+        for j, owner in enumerate(self.order):
+            theirs = part.at[rows(1 - side, owner), :]
+            self.pairs.append(
+                remote("grid", pair, theirs, paired.at[j], pair_s.at[j], pair_r.at[j])
             )
-            self.back.append(
-                remote("grid", peer, mine, target.at[self.own, :], s2.at[k - 1], r2.at[k - 1])
+            done = target.at[self.mine[j], :]
+            source = own if j == self.last else done
+            self.passed.append(remote("grid", pair, source, done, pass_s.at[j], pass_r.at[j]))
+            if j == self.last:
+                continue
+            peer = 2 * owner + side
+            here = middle.at[j]
+            self.far.append(
+                remote("grid", peer, here, arrived.at[place], far_s.at[j], far_r.at[place])
             )
+            self.far_in.append(
+                remote("grid", peer, here, arrived.at[owner], far_s.at[j], far_r.at[owner])
+            )
+            home = target.at[rows(side, place), :]
+            self.back.append(remote("grid", peer, own, home, back_s.at[j], back_r.at[place]))
+            self.back_in.append(remote("grid", peer, own, done, back_s.at[j], back_r.at[owner]))
 
     def scatter(self):
-        for copy in self.out:
+        for copy in self.pairs:
             copy.start()
 
+    def middle(self):
+        for j, copy in enumerate(self.pairs):
+            copy.wait_recv()
+            self.held[j] = self.part[self.mine[j], :] + self.paired[j]
+            if j < self.last:
+                self.far[j].start()
+
     def add(self):
-        total = self.part[self.own, :]
-        for k, copy in enumerate(self.out):
-            copy.wait_recv()
-            total = total + self.arrived[k]
-        self.mine[...] = total
+        total = self.held[self.last]
+        for j in reversed(range(self.last)):
+            self.far_in[j].wait_recv()
+            total = total + self.arrived[self.order[j]]
+        self.held[self.last] = total
         for copy in self.back:
             copy.start()
-        self.target[self.own, :] = total
+        self.passed[self.last].start()
+        self.target[self.mine[self.last], :] = total
+
+    def relay(self):
+        for j in reversed(range(self.last)):
+            self.back_in[j].wait_recv()
+            self.passed[j].start()
 
     def finish(self):
-        for copy in self.back:
+        for copy in reversed(self.passed):
             copy.wait_recv()
-        for copy in self.out + self.back:
+        for copy in self.pairs + self.far + self.back + self.passed:
             copy.wait_send()
 
 
@@ -208,7 +256,7 @@
     (u0, x0, pot, out_ref, quot_ref, norm_ref) = refs[:6]
     (
         u, xr, kk, wb, uh, um, ul, xh, xm, kh, km, lh, lm, ll, work, panel, spread,
-        spart, cpart, sin, cin, smine, cmine, csum, sall, hz, hs, hr, stat, stats, lam,
+        spart, cpart, spair, cpair, sin, cin, smid, cmid, csum, sall, hz, hs, hr, stat, stats, lam,
         sums_s, sums_c, gat_u, gat_x, gat_s, gat_k, halo_z, halo_y, stat_s, stat_r,
     ) = refs[6:]
     me = lax.axis_index("grid")
@@ -241,6 +289,7 @@
     gather_u.pass_on()
     gather_u.finish()
 
+    peers = far_first(me, count)
     odd = lax.rem(me, 2)
     z_peer = lax.rem(me + count + 4 * odd - 2, count)
     y_peer = me + 1 - 2 * odd
@@ -258,8 +307,8 @@
                     target[rows, lanes(j)] = piece
 
     def iteration(it):
-        sum_s = GridSum(spart, sin, smine, sall.at[band], me, count, [sums_s.at[i] for i in range(4)])
-        sum_c = GridSum(cpart, cin, cmine, csum, me, count, [sums_c.at[i] for i in range(4)])
+        sum_s = GridSum(spart, spair, sin, smid, sall.at[band], me, count, [sums_s.at[i] for i in range(8)])
+        sum_c = GridSum(cpart, cpair, cin, cmid, csum, me, count, [sums_c.at[i] for i in range(8)])
         gather_s = BandGather(
             sall.at[band].reshape(1, total, w), sall.reshape(bands, 1, total, w), place,
             (gat_s.at[0], gat_s.at[1]),
@@ -287,7 +336,6 @@
                 at = start + c * w
                 spart[at : at + w, :] = tile[:, lanes(c)]
         sum_s.scatter()
-        across_z[1].start()
 
         @pl.when(it == 0)
         def _():
@@ -301,6 +349,25 @@
             for c in range(WIDE // w):
                 at = start + c * w
                 cpart[at : at + w, :] = tile[:, lanes(c)]
+
+        @pl.loop(0, nx)
+        def _(x):
+            def rows_at(at):
+                return pl.ds(pl.multiple_of(lax.rem(at + nx, nx) * ny, ny), ny)
+
+            rows = rows_at(x)
+            field = [u[band, p, rows, :] for p in range(planes)]
+            for p in range(planes):
+                value = 3.0 * STENCIL[0] * field[p]
+                for d in range(1, 5):
+                    near = u[band, p, rows_at(x + d), :] + u[band, p, rows_at(x - d), :]
+                    near = near + pltpu.roll(field[p], d, 0) + pltpu.roll(field[p], ny - d, 0)
+                    if p - d >= 0:
+                        near = near + field[p - d]
+                    if p + d < planes:
+                        near = near + field[p + d]
+                    value = value + STENCIL[d] * near
+                kk[band, p, rows, :] = -0.5 * value + pot[p, rows, :] * field[p]
 
         def halo_part(q):
             across_z[q].wait_recv()
@@ -327,44 +394,29 @@
                             hs[p, rows, :] = value
             across_y[q].start()
 
+        sum_s.middle()
+        halo_part(0)
         sum_s.add()
         sum_c.scatter()
+        sum_s.relay()
+        sum_c.middle()
+        across_z[1].start()
         across_z[2].start()
         across_z[3].start()
-        halo_part(0)
-        halo_part(1)
-
-        @pl.loop(0, nx)
-        def _(x):
-            def rows_at(at):
-                return pl.ds(pl.multiple_of(lax.rem(at + nx, nx) * ny, ny), ny)
-
-            rows = rows_at(x)
-            field = [u[band, p, rows, :] for p in range(planes)]
-            for p in range(planes):
-                value = 3.0 * STENCIL[0] * field[p]
-                for d in range(1, 5):
-                    near = u[band, p, rows_at(x + d), :] + u[band, p, rows_at(x - d), :]
-                    near = near + pltpu.roll(field[p], d, 0) + pltpu.roll(field[p], ny - d, 0)
-                    if p - d >= 0:
-                        near = near + field[p - d]
-                    if p + d < planes:
-                        near = near + field[p + d]
-                    value = value + STENCIL[d] * near
-                kk[band, p, rows, :] = -0.5 * value + pot[p, rows, :] * field[p]
-
         sum_s.finish()
         gather_s.start()
+        halo_part(1)
+        gather_s.pass_on()
+        sum_c.add()
         halo_part(2)
         halo_part(3)
-        sum_c.add()
-        gather_s.pass_on()
         gather_s.finish()
         for b in range(bands):
             for c in range(bands):
                 work[b * w : (b + 1) * w, lanes(c)] = sall[b, c * w : (c + 1) * w, :]
 
         def exchange_and_send():
+            sum_c.relay()
             sum_c.finish()
             coupling = jnp.concatenate(
                 [jnp.transpose(csum[c * w : (c + 1) * w, :]) for c in range(bands)], axis=0
@@ -397,11 +449,15 @@
                     panel[:, there], work[here, :], ((0,), (0,))
                 )
 
-            @pl.when(k == 1)
+            @pl.when(k == 0)
             def _():
                 exchange_and_send()
 
-        gather_k.pass_on()
+            @pl.when(k == bands - 2)
+            def _():
+                gather_k.pass_on(0, PIECES // 2)
+
+        gather_k.pass_on(PIECES // 2, PIECES)
         for r in range(bands):
             rows = slice(r * w, (r + 1) * w)
             for target, piece in zip((lh, lm, ll), split(work[rows, :], 3)):
@@ -453,14 +509,15 @@
             stat[2 * bands + j : 2 * bands + j + 1, :] = rest
 
         copies = []
-        for k in range(1, count):
-            peer = lax.rem(me + k, count)
-            copy = remote("grid", peer, stat, stats.at[me], stat_s.at[k - 1], stat_r.at[k - 1])
+        for k, peer in enumerate(peers):
+            copy = remote("grid", peer, stat, stats.at[me], stat_s.at[k], stat_r.at[me])
             copy.start()
             copies.append(copy)
         stats[me] = stat[...]
+        for k, peer in enumerate(peers):
+            remote("grid", peer, stat, stats.at[peer], stat_s.at[k], stat_r.at[peer]).wait_recv()
         for copy in copies:
-            copy.wait()
+            copy.wait_send()
         quotient = stats[0, :bands, :]
         for c in range(1, count):
             quotient = quotient + stats[c, :bands, :]
@@ -506,8 +563,7 @@
     half = pltpu.VMEM((n, total), BF16)
     square = pltpu.VMEM((total, total), BF16)
     column = pltpu.VMEM((total, w), F32)
-    arrived = pltpu.VMEM((count - 1, chunk, w), F32)
-    mine = pltpu.VMEM((chunk, w), F32)
+    chunks = pltpu.VMEM((count // 2, chunk, w), F32)
     slab = pltpu.VMEM(field, F32)
     dma = pltpu.SemaphoreType.DMA
     spread_potential = jnp.broadcast_to(potential.reshape(planes, plane, 1), field)
@@ -525,17 +581,17 @@
             pltpu.VMEM((w, total), F32),
             pltpu.VMEM((2, 72, w), F32),
         ]
-        + [column, column, arrived, arrived, mine, mine, column]
+        + [column, column] + [chunks] * 6 + [column]
         + [pltpu.VMEM((bands, total, w), F32), slab, slab, slab]
         + [
             pltpu.VMEM((16, w), F32),
             pltpu.VMEM((count, 16, w), F32),
             pltpu.VMEM((3, 8, w), F32),
         ]
-        + [dma((4, count - 1))] * 2
+        + [dma((8, count // 2))] * 2
         + [dma((2, 3, PIECES))] * 4
         + [dma((2, PIECES))] * 2
-        + [dma((count - 1,))] * 2,
+        + [dma((count,))] * 2,
         compiler_params=pltpu.CompilerParams(
             collective_id=0, has_side_effects=True, vmem_limit_bytes=60 * 2**20
         ),

time: 249 us -> 222 us (0.89)
  Pallas kernels: 243 us -> 216 us
    pallas_call x1, Pallas kernels: 243 us -> 216 us  [local(): pl.pallas_call(functools.partial(iterations_kernel, count, bands, ny), ou...]
where the time goes in v3:
time: 222 us
  Pallas kernels  216 us (97%)
  local copies, waits for them, and re-layouts  4.97 us (2%)
    pallas_call x1, Pallas kernels, local(): pl.pallas_call(functools.partial(iterations_kernel, count, bands, ny), ou...  216 us

profile of v3, /device:TPU:0, one launch (start us, length us, event | category | flops | bytes accessed | tf_op | source)
XLA Modules:
  0.0 221.6 jit_solution(1391817470525651343)
XLA Ops:
  0.6 0.8 broadcast_in_dim.7
  1.5 1.0 broadcast_in_dim.8.refs_2_
  2.5 216.0 %shard_map.58 = (f32[4,256,128]{2,1,0:T(8,128)}, f32[3,128]{1,0:T(4,128)}, f32[3,128]{1,0:T(4,128)}) custom-call(f32[4,256,128]{2,1,0:T(8,128)} %bitcast.3, f32[4,256,128]{2,1,0:T(8,128)} %bitcast.4, f32[4,256,128]{2,1,0:T(8,128)} %broadcast_in_dim.8.refs_2_), custom_call_target="tpu_custom_call" | custom-call | tf_op jit(solution)/shard_map/pallas_call | solution.py:571
  218.5 0.0 copy-start.1
  218.5 1.9 copy.9
  220.3 0.0 copy-done.1
  220.3 0.0 copy-start
  220.3 0.6 copy.10
  220.9 0.1 copy-done
  221.0 0.6 copy.11
Async XLA Ops:
  218.5 1.9 copy-start.1
  220.3 0.7 copy-start

commit v4 on v3

--- a/solution.py
+++ b/solution.py
@@ -126,13 +126,11 @@
 
 
 class BandGather:
-    def __init__(self, source, target, place, sems):
+    def __init__(self, source, target, place, parts, sems):
         send, recv = sems
         me, partner, across = place
         self.copies = []
-        rows = target.shape[2] // PIECES
-        for q in range(PIECES):
-            part = pl.ds(q * rows, rows)
+        for q, part in enumerate(parts):
 
             def block(owner, part=part):
                 return target.at[owner, :, part, :]
@@ -145,16 +143,16 @@
             )
             self.copies.append((far, near, relay))
 
-    def start(self):
-        for far, _, _ in self.copies:
-            far.start()
-        for _, near, _ in self.copies:
-            near.start()
-
-    def pass_on(self, first=0, last=PIECES):
-        for far, _, relay in self.copies[first:last]:
-            far.wait_recv()
-            relay.start()
+    def send(self, *which):
+        for q in which:
+            self.copies[q][0].start()
+        for q in which:
+            self.copies[q][1].start()
+
+    def pass_on(self, *which):
+        for q in which:
+            self.copies[q][0].wait_recv()
+            self.copies[q][2].start()
 
     def finish(self):
         for far, near, relay in self.copies:
@@ -178,7 +176,7 @@
 
 
 class GridSum:
-    def __init__(self, part, paired, arrived, middle, target, me, count, sems):
+    def __init__(self, part, paired, arrived, middle, target, me, count, sems, ready=None):
         pair_s, pair_r, far_s, far_r, back_s, back_r, pass_s, pass_r = sems
         self.part, self.paired, self.arrived, self.held, self.target = (
             part, paired, arrived, middle, target,
@@ -189,11 +187,13 @@
         pair = me + 1 - 2 * side
         self.order = far_first(place, half) + [place]
         self.last = half - 1
+        self.ready = ready
 
         def rows(parity, owner):
             return pl.ds(pl.multiple_of((parity * half + owner) * chunk, chunk), chunk)
 
         self.mine = [rows(side, owner) for owner in self.order]
+        self.parts = self.mine + [rows(1 - side, owner) for owner in self.order]
         self.pairs, self.far, self.far_in, self.back, self.back_in, self.passed = [], [], [], [], [], []
         own = middle.at[self.last]
         for j, owner in enumerate(self.order):
@@ -239,15 +239,21 @@
             copy.start()
         self.passed[self.last].start()
         self.target[self.mine[self.last], :] = total
+        if self.ready:
+            self.ready(self.last)
 
     def relay(self):
         for j in reversed(range(self.last)):
             self.back_in[j].wait_recv()
             self.passed[j].start()
+            if self.ready:
+                self.ready(j)
 
     def finish(self):
-        for copy in reversed(self.passed):
-            copy.wait_recv()
+        for j in reversed(range(self.last + 1)):
+            self.passed[j].wait_recv()
+            if self.ready:
+                self.ready(self.last + 1 + j)
         for copy in self.pairs + self.far + self.back + self.passed:
             copy.wait_send()
 
@@ -255,7 +261,7 @@
 def iterations_kernel(count, bands, ny, *refs):
     (u0, x0, pot, out_ref, quot_ref, norm_ref) = refs[:6]
     (
-        u, xr, kk, wb, uh, um, ul, xh, xm, kh, km, lh, lm, ll, work, panel, spread,
+        u, xr, kk, wb, uh, um, ul, xh, xm, kh, km, lh, lm, work, spread,
         spart, cpart, spair, cpair, sin, cin, smid, cmid, csum, sall, hz, hs, hr, stat, stats, lam,
         sums_s, sums_c, gat_u, gat_x, gat_s, gat_k, halo_z, halo_y, stat_s, stat_r,
     ) = refs[6:]
@@ -280,20 +286,22 @@
     pl.semaphore_wait(barrier, count + 1)
 
     stat[...] = jnp.zeros_like(stat)
-    gather_u = BandGather(u0, u, place, (gat_u.at[0], gat_u.at[1]))
-    gather_x = BandGather(x0, xr, place, (gat_x.at[0], gat_x.at[1]))
-    gather_u.start()
-    gather_x.start()
+    part_rows = plane // PIECES
+    parts = [pl.ds(q * part_rows, part_rows) for q in range(PIECES)]
+    every = range(PIECES)
+    gather_u = BandGather(u0, u, place, parts, (gat_u.at[0], gat_u.at[1]))
+    gather_x = BandGather(x0, xr, place, parts, (gat_x.at[0], gat_x.at[1]))
+    gather_u.send(*every)
+    gather_x.send(*every)
     u[band] = u0[...]
     xr[band] = x0[...]
-    gather_u.pass_on()
+    gather_u.pass_on(*every)
     gather_u.finish()
 
     peers = far_first(me, count)
     odd = lax.rem(me, 2)
     z_peer = lax.rem(me + count + 4 * odd - 2, count)
     y_peer = me + 1 - 2 * odd
-    part_rows = plane // PIECES
 
     def lanes(j):
         return slice(j * w, (j + 1) * w)
@@ -311,12 +319,16 @@
         sum_c = GridSum(cpart, cpair, cin, cmid, csum, me, count, [sums_c.at[i] for i in range(8)])
         gather_s = BandGather(
             sall.at[band].reshape(1, total, w), sall.reshape(bands, 1, total, w), place,
-            (gat_s.at[0], gat_s.at[1]),
+            sum_s.parts, (gat_s.at[0], gat_s.at[1]),
         )
-        gather_k = BandGather(kk.at[band], kk, place, (gat_k.at[0], gat_k.at[1]))
+        sum_s.ready = gather_s.send
+        last = sum_s.last
+        first_half = list(reversed(range(last + 1)))
+        second_half = [last + 1 + j for j in first_half]
+        gather_k = BandGather(kk.at[band], kk, place, parts, (gat_k.at[0], gat_k.at[1]))
         across_z, across_y = [], []
         for q in range(PIECES):
-            part = pl.ds(q * part_rows, part_rows)
+            part = parts[q]
             across_z.append(
                 remote("grid", z_peer, u.at[band, :, part, :], hz.at[:, part, :],
                        halo_z.at[0, q], halo_z.at[1, q])
@@ -337,18 +349,13 @@
                 spart[at : at + w, :] = tile[:, lanes(c)]
         sum_s.scatter()
 
-        @pl.when(it == 0)
-        def _():
-            gather_x.pass_on()
-            gather_x.finish()
-            split_blocks(xr, (xh, xm))
-
-        for start in range(0, total, WIDE):
-            wide = slice(start, start + WIDE)
-            tile = split_dot(turned[:2], [xh[:, wide], xm[:, wide]], ((1,), (0,)))
-            for c in range(WIDE // w):
-                at = start + c * w
-                cpart[at : at + w, :] = tile[:, lanes(c)]
+        def couple():
+            for start in range(0, total, WIDE):
+                wide = slice(start, start + WIDE)
+                tile = split_dot(turned[:2], [xh[:, wide], xm[:, wide]], ((1,), (0,)))
+                for c in range(WIDE // w):
+                    at = start + c * w
+                    cpart[at : at + w, :] = tile[:, lanes(c)]
 
         @pl.loop(0, nx)
         def _(x):
@@ -395,118 +402,178 @@
             across_y[q].start()
 
         sum_s.middle()
+
+        @pl.when(it > 0)
+        def _():
+            couple()
+
+        sum_s.add()
+
+        @pl.when(it == 0)
+        def _():
+            gather_x.pass_on(*every)
+            gather_x.finish()
+            split_blocks(xr, (xh, xm))
+            couple()
+
+        sum_c.scatter()
         halo_part(0)
-        sum_s.add()
-        sum_c.scatter()
         sum_s.relay()
         sum_c.middle()
         across_z[1].start()
+        sum_s.finish()
+        gather_s.pass_on(*first_half)
+        gather_s.pass_on(*second_half)
+        sum_c.add()
         across_z[2].start()
         across_z[3].start()
-        sum_s.finish()
-        gather_s.start()
-        halo_part(1)
-        gather_s.pass_on()
-        sum_c.add()
-        halo_part(2)
-        halo_part(3)
         gather_s.finish()
         for b in range(bands):
             for c in range(bands):
                 work[b * w : (b + 1) * w, lanes(c)] = sall[b, c * w : (c + 1) * w, :]
 
-        def exchange_and_send():
-            sum_c.relay()
+        def exchange():
             sum_c.finish()
             coupling = jnp.concatenate(
                 [jnp.transpose(csum[c * w : (c + 1) * w, :]) for c in range(bands)], axis=0
             )
             right = split(coupling, 2)
-            for copy in across_y:
-                copy.wait_recv()
 
             @pl.loop(0, planes)
             def _(p):
                 rows = pl.ds(pl.multiple_of(p * plane, plane), plane)
-                exchange = split_dot([xh[rows, :], xm[rows, :]], right, ((1,), (0,)))
-                kk[band, p] = kk[band, p] - 0.5 * hr[p] - exchange
-            gather_k.start()
-
-        @pl.loop(0, bands)
-        def _(k):
-            here = pl.ds(pl.multiple_of(k * w, w), w)
-            inverse = block_inverse_factor(work[here, here], spread)
-            rows = exact_dot(inverse, work[here, :], ((1,), (0,)))
-            panel[...] = rows
-            work[here, :] = rows
-            work[here, here] = inverse
-
-            @pl.loop(k + 1, bands)
-            def _(i):
-                there = pl.ds(pl.multiple_of(i * w, w), w)
-                work[there, here] = jnp.zeros((w, w), F32)
-                work[there, :] = work[there, :] - exact_dot(
-                    panel[:, there], work[here, :], ((0,), (0,))
+                change = split_dot([xh[rows, :], xm[rows, :]], right, ((1,), (0,)))
+                kk[band, p] = kk[band, p] - change
+
+        def send_k(q):
+            across_y[q].wait_recv()
+            for p in range(planes):
+                kk[band, p, parts[q], :] = kk[band, p, parts[q], :] - 0.5 * hr[p, parts[q], :]
+            gather_k.send(q)
+
+        def service(k):
+            if k == 0:
+                sum_c.relay()
+                halo_part(1)
+            if k == 1:
+                halo_part(2)
+                exchange()
+                send_k(0)
+                send_k(1)
+            if k == 2:
+                halo_part(3)
+                send_k(2)
+            if k == 3:
+                send_k(3)
+                gather_k.pass_on(0, 1)
+
+        def rows_of(k):
+            return slice(k * w, (k + 1) * w)
+
+        inverse = block_inverse_factor(work[rows_of(0), rows_of(0)], spread)
+        for k in range(bands - 1):
+            service(k)
+            here, after = rows_of(k), rows_of(k + 1)
+            step = exact_dot(inverse, work[here, after], ((1,), (0,)))
+            pivot = work[after, after] - exact_dot(step, step, ((0,), (0,)))
+            following = block_inverse_factor(pivot, spread)
+            rows = exact_dot(inverse, work[here, (k + 1) * w :], ((1,), (0,)))
+            left = inverse
+            if k:
+                left = jnp.concatenate(
+                    [exact_dot(inverse, work[here, : k * w], ((1,), (0,))), inverse], axis=1
                 )
-
-            @pl.when(k == 0)
-            def _():
-                exchange_and_send()
-
-            @pl.when(k == bands - 2)
-            def _():
-                gather_k.pass_on(0, PIECES // 2)
-
-        gather_k.pass_on(PIECES // 2, PIECES)
+            work[here, : (k + 1) * w] = left
+            for i in range(k + 1, bands):
+                turn = rows[:, (i - k - 1) * w : (i - k) * w]
+                if i > k + 1:
+                    work[rows_of(i), i * w :] = work[rows_of(i), i * w :] - exact_dot(
+                        turn, rows[:, (i - k - 1) * w :], ((0,), (0,))
+                    )
+                if i + 1 < bands and i == k + 1:
+                    work[rows_of(i), (i + 1) * w :] = work[rows_of(i), (i + 1) * w :] - exact_dot(
+                        turn, rows[:, w:], ((0,), (0,))
+                    )
+                change = exact_dot(turn, left, ((0,), (0,)))
+                if k:
+                    work[rows_of(i), : k * w] = work[rows_of(i), : k * w] - change[:, : k * w]
+                work[rows_of(i), here] = -change[:, k * w :]
+            inverse = following
+        service(bands - 1)
+        here = rows_of(bands - 1)
+        left = exact_dot(inverse, work[here, : (bands - 1) * w], ((1,), (0,)))
+        work[here, :] = jnp.concatenate([left, inverse], axis=1)
         for r in range(bands):
-            rows = slice(r * w, (r + 1) * w)
-            for target, piece in zip((lh, lm, ll), split(work[rows, :], 3)):
-                target[rows, : (r + 1) * w] = piece[:, : (r + 1) * w]
+            rows = rows_of(r)
+            for target, piece in zip((lh, lm), split(work[rows, : (r + 1) * w], 2)):
+                target[rows, : (r + 1) * w] = piece
                 if (r + 1) * w < total:
                     target[rows, (r + 1) * w :] = jnp.zeros((w, total - (r + 1) * w), BF16)
+        gather_k.pass_on(2, 3)
         gather_k.finish()
         split_blocks(kk, (kh, km))
         for copy in across_z + across_y:
             copy.wait_send()
 
-        @pl.loop(0, planes)
-        def _(p):
-            rows = pl.ds(pl.multiple_of(p * plane, plane), plane)
-            for start in range(0, total, WIDE):
-                deep = slice(0, start + WIDE)
-                wide = slice(start, start + WIDE)
-                right = [lh[wide, deep], lm[wide, deep], ll[wide, deep]]
-                v = split_dot([uh[rows, deep], um[rows, deep], ul[rows, deep]], right, ((1,), (1,)))
-                t = split_dot([kh[rows, deep], km[rows, deep]], right[:2], ((1,), (1,)))
-                for c in range(WIDE // w):
-                    u[start // w + c, p] = v[:, lanes(c)]
-                    wb[start // w + c, p] = t[:, lanes(c)]
-
         def column_sum(value):
             return jnp.sum(value, axis=0, keepdims=True)
 
         def eight(value):
             return jnp.sum(value.reshape(plane // 8, 8, w), axis=0)
 
-        for j in range(bands):
-            zero = jnp.zeros((8, w), F32)
-
-            def first(p, carry, j=j):
-                v, t = u[j, p], wb[j, p]
-                return carry[0] + eight(v * t), carry[1] + eight(v * v)
-
-            vw, vv = lax.fori_loop(0, planes, first, (zero, zero))
+        def apply(p, sums, which, places, deep):
+            rows = pl.ds(pl.multiple_of(p * plane, plane), plane)
+            right = [lh[which, deep], lm[which, deep]]
+            v = split_dot([uh[rows, deep], um[rows, deep]], right, ((1,), (1,)))
+            t = split_dot([kh[rows, deep], km[rows, deep]], right, ((1,), (1,)))
+            out = []
+            for c, (j, (vw, vv)) in enumerate(zip(places, sums)):
+                vj, tj = v[:, lanes(c)], t[:, lanes(c)]
+                u[j, p] = vj
+                wb[j, p] = tj
+                out.append((vw + eight(vj * tj), vv + eight(vj * vj)))
+            return out
+
+        def record(j, vw, vv):
             vw, vv = column_sum(vw), column_sum(vv)
             slope = jnp.where(vv > 1e-12, vw / jnp.maximum(vv, 1e-12), 0.0)
 
-            def second(p, carry, j=j, slope=slope):
+            def second(p, carry):
                 r = wb[j, p] - slope * u[j, p]
                 return carry + eight(r * r)
 
             rest = column_sum(lax.fori_loop(0, planes, second, zero))
-            stat[j : j + 1, :] = vw
-            stat[bands + j : bands + j + 1, :] = vv
-            stat[2 * bands + j : 2 * bands + j + 1, :] = rest
+            stat[pl.ds(j, 1), :] = vw
+            stat[pl.ds(bands + j, 1), :] = vv
+            stat[pl.ds(2 * bands + j, 1), :] = rest
+
+        zero = jnp.zeros((8, w), F32)
+
+        @pl.when(it < ITERS - 1)
+        def _():
+            def body(p, sums):
+                out = []
+                for start in range(0, total, WIDE):
+                    places = range(start // w, (start + WIDE) // w)
+                    out += apply(
+                        p, [sums[j] for j in places], slice(start, start + WIDE), places,
+                        slice(0, start + WIDE),
+                    )
+                return tuple(out)
+
+            sums = lax.fori_loop(0, planes, body, ((zero, zero),) * bands)
+            for j in range(bands):
+                record(j, *sums[j])
+
+        @pl.when(it == ITERS - 1)
+        def _():
+            which = pl.ds(pl.multiple_of(band * w, w), w)
+
+            def body(p, sums):
+                return apply(p, [sums], which, [band], slice(0, total))[0]
+
+            vw, vv = lax.fori_loop(0, planes, body, (zero, zero))
+            record(band, vw, vv)
 
         copies = []
         for k, peer in enumerate(peers):
@@ -534,13 +601,22 @@
         lam[2, :bands, :] = STEP_LENGTH / jnp.sqrt(squared + NORM_EPS)
         quot_ref[pl.ds(it, 1), :] = lam[0, pl.ds(band, 1), :]
         norm_ref[pl.ds(it, 1), :] = lam[1, pl.ds(band, 1), :]
-        for j in range(bands):
-            rate, length = lam[0, j : j + 1, :], lam[2, j : j + 1, :]
+        def renew(j):
+            rate, length = lam[0, pl.ds(j, 1), :], lam[2, pl.ds(j, 1), :]
 
             @pl.loop(0, planes)
-            def _(p, j=j, rate=rate, length=length):
+            def _(p):
                 v = u[j, p]
                 u[j, p] = v - (wb[j, p] - rate * v) * length
+
+        @pl.when(it < ITERS - 1)
+        def _():
+            for j in range(bands):
+                renew(j)
+
+        @pl.when(it == ITERS - 1)
+        def _():
+            renew(band)
 
     @pl.loop(0, ITERS)
     def _(it):
@@ -575,10 +651,9 @@
         out_specs=(VMEM, VMEM, VMEM),
         scratch_shapes=[block] * 4
         + [half] * 7
-        + [square] * 3
+        + [square] * 2
         + [
             pltpu.VMEM((total, total), F32),
-            pltpu.VMEM((w, total), F32),
             pltpu.VMEM((2, 72, w), F32),
         ]
         + [column, column] + [chunks] * 6 + [column]
@@ -589,7 +664,8 @@
             pltpu.VMEM((3, 8, w), F32),
         ]
         + [dma((8, count // 2))] * 2
-        + [dma((2, 3, PIECES))] * 4
+        + [dma((2, 3, PIECES))] * 2
+        + [dma((2, 3, count)), dma((2, 3, PIECES))]
         + [dma((2, PIECES))] * 2
         + [dma((count,))] * 2,
         compiler_params=pltpu.CompilerParams(

time: 222 us -> 204 us (0.919)
  Pallas kernels: 216 us -> 198 us
    pallas_call x1, Pallas kernels: 216 us -> 198 us  [local(): pl.pallas_call(functools.partial(iterations_kernel, count, bands, ny), ou...]
where the time goes in v4:
time: 204 us; the launch traced here: 203 us
  Pallas kernels  198 us (97%)
  local copies, waits for them, and re-layouts  4.97 us (2%)
    pallas_call x1, Pallas kernels, local(): pl.pallas_call(functools.partial(iterations_kernel, count, bands, ny), ou...  198 us

profile of v4, /device:TPU:0, one launch (start us, length us, event | category | flops | bytes accessed | tf_op | source)
XLA Modules:
  0.0 203.3 jit_solution(16764760003283426913)
XLA Ops:
  0.6 0.8 broadcast_in_dim.7
  1.5 1.0 broadcast_in_dim.8.refs_2_
  2.5 197.7 %shard_map.58 = (f32[4,256,128]{2,1,0:T(8,128)}, f32[3,128]{1,0:T(4,128)}, f32[3,128]{1,0:T(4,128)}) custom-call(f32[4,256,128]{2,1,0:T(8,128)} %bitcast.3, f32[4,256,128]{2,1,0:T(8,128)} %bitcast.4, f32[4,256,128]{2,1,0:T(8,128)} %broadcast_in_dim.8.refs_2_), custom_call_target="tpu_custom_call" | custom-call | tf_op jit(solution)/shard_map/pallas_call | solution.py:647
  200.2 0.0 copy-start.1
  200.2 1.9 copy.9
  202.0 0.0 copy-done.1
  202.0 0.0 copy-start
  202.0 0.6 copy.10
  202.6 0.1 copy-done
  202.7 0.6 copy.11
Async XLA Ops:
  200.2 1.9 copy-start.1
  202.0 0.7 copy-start

commit v5 on v4

--- a/solution.py
+++ b/solution.py
@@ -52,7 +52,7 @@
     return total
 
 
-def block_inverse_factor(block, spread):
+def block_inverse_factor(block, spread, pause):
     size = block.shape[0]
     count = size // 8
     groups = [block[8 * g : 8 * g + 8, :] for g in range(count)]
@@ -64,6 +64,8 @@
 
     finished = []
     for g in range(count):
+        if g == count // 2:
+            pause()
         first = 8 * g
         slot = g % 2
         inside = (lane >= first) & (lane < first + 8)
@@ -261,9 +263,9 @@
 def iterations_kernel(count, bands, ny, *refs):
     (u0, x0, pot, out_ref, quot_ref, norm_ref) = refs[:6]
     (
-        u, xr, kk, wb, uh, um, ul, xh, xm, kh, km, lh, lm, work, spread,
-        spart, cpart, spair, cpair, sin, cin, smid, cmid, csum, sall, hz, hs, hr, stat, stats, lam,
-        sums_s, sums_c, gat_u, gat_x, gat_s, gat_k, halo_z, halo_y, stat_s, stat_r,
+        u, xr, kk, wb, uh, um, ul, xh, xm, kh, km, lh, lm, mh, mm, gh, gm, work, spread,
+        spart, cpart, spair, cpair, sin, cin, smid, cmid, call, sall, hz, hs, hr, stat, stats, lam,
+        sums_s, sums_c, gat_u, gat_x, gat_s, gat_c, gat_k, halo_z, halo_y, stat_s, stat_r,
     ) = refs[6:]
     me = lax.axis_index("grid")
     band = lax.axis_index("band")
@@ -316,7 +318,7 @@
 
     def iteration(it):
         sum_s = GridSum(spart, spair, sin, smid, sall.at[band], me, count, [sums_s.at[i] for i in range(8)])
-        sum_c = GridSum(cpart, cpair, cin, cmid, csum, me, count, [sums_c.at[i] for i in range(8)])
+        sum_c = GridSum(cpart, cpair, cin, cmid, call.at[band], me, count, [sums_c.at[i] for i in range(8)])
         gather_s = BandGather(
             sall.at[band].reshape(1, total, w), sall.reshape(bands, 1, total, w), place,
             sum_s.parts, (gat_s.at[0], gat_s.at[1]),
@@ -325,6 +327,10 @@
         last = sum_s.last
         first_half = list(reversed(range(last + 1)))
         second_half = [last + 1 + j for j in first_half]
+        gather_c = BandGather(
+            call.at[band].reshape(1, total, w), call.reshape(bands, 1, total, w), place,
+            sum_c.parts, (gat_c.at[0], gat_c.at[1]),
+        )
         gather_k = BandGather(kk.at[band], kk, place, parts, (gat_k.at[0], gat_k.at[1]))
         across_z, across_y = [], []
         for q in range(PIECES):
@@ -421,30 +427,17 @@
         sum_s.relay()
         sum_c.middle()
         across_z[1].start()
+        across_z[2].start()
         sum_s.finish()
         gather_s.pass_on(*first_half)
         gather_s.pass_on(*second_half)
         sum_c.add()
-        across_z[2].start()
         across_z[3].start()
         gather_s.finish()
         for b in range(bands):
             for c in range(bands):
                 work[b * w : (b + 1) * w, lanes(c)] = sall[b, c * w : (c + 1) * w, :]
 
-        def exchange():
-            sum_c.finish()
-            coupling = jnp.concatenate(
-                [jnp.transpose(csum[c * w : (c + 1) * w, :]) for c in range(bands)], axis=0
-            )
-            right = split(coupling, 2)
-
-            @pl.loop(0, planes)
-            def _(p):
-                rows = pl.ds(pl.multiple_of(p * plane, plane), plane)
-                change = split_dot([xh[rows, :], xm[rows, :]], right, ((1,), (0,)))
-                kk[band, p] = kk[band, p] - change
-
         def send_k(q):
             across_y[q].wait_recv()
             for p in range(planes):
@@ -453,30 +446,41 @@
 
         def service(k):
             if k == 0:
-                sum_c.relay()
                 halo_part(1)
             if k == 1:
+                sum_c.ready = gather_c.send
+                gather_c.send(last)
+                sum_c.relay()
+                send_k(0)
                 halo_part(2)
-                exchange()
-                send_k(0)
-                send_k(1)
             if k == 2:
                 halo_part(3)
+            if k == 3:
+                sum_c.finish()
+                send_k(1)
+            if k == 4:
                 send_k(2)
-            if k == 3:
+                gather_c.pass_on(*first_half)
+            if k == 5:
+                gather_c.pass_on(*second_half)
                 send_k(3)
+            if k == 6:
                 gather_k.pass_on(0, 1)
+            if k == 7:
+                gather_k.pass_on(2)
+                gather_c.finish()
 
         def rows_of(k):
             return slice(k * w, (k + 1) * w)
 
-        inverse = block_inverse_factor(work[rows_of(0), rows_of(0)], spread)
+        inverse = block_inverse_factor(
+            work[rows_of(0), rows_of(0)], spread, functools.partial(service, 0)
+        )
         for k in range(bands - 1):
-            service(k)
+            service(2 * k + 1)
             here, after = rows_of(k), rows_of(k + 1)
             step = exact_dot(inverse, work[here, after], ((1,), (0,)))
             pivot = work[after, after] - exact_dot(step, step, ((0,), (0,)))
-            following = block_inverse_factor(pivot, spread)
             rows = exact_dot(inverse, work[here, (k + 1) * w :], ((1,), (0,)))
             left = inverse
             if k:
@@ -486,20 +490,17 @@
             work[here, : (k + 1) * w] = left
             for i in range(k + 1, bands):
                 turn = rows[:, (i - k - 1) * w : (i - k) * w]
-                if i > k + 1:
-                    work[rows_of(i), i * w :] = work[rows_of(i), i * w :] - exact_dot(
-                        turn, rows[:, (i - k - 1) * w :], ((0,), (0,))
-                    )
-                if i + 1 < bands and i == k + 1:
-                    work[rows_of(i), (i + 1) * w :] = work[rows_of(i), (i + 1) * w :] - exact_dot(
-                        turn, rows[:, w:], ((0,), (0,))
+                begin = max(i, k + 2)
+                if begin < bands:
+                    work[rows_of(i), begin * w :] = work[rows_of(i), begin * w :] - exact_dot(
+                        turn, rows[:, (begin - k - 1) * w :], ((0,), (0,))
                     )
                 change = exact_dot(turn, left, ((0,), (0,)))
                 if k:
                     work[rows_of(i), : k * w] = work[rows_of(i), : k * w] - change[:, : k * w]
                 work[rows_of(i), here] = -change[:, k * w :]
-            inverse = following
-        service(bands - 1)
+            inverse = block_inverse_factor(pivot, spread, functools.partial(service, 2 * k + 2))
+        service(2 * bands - 1)
         here = rows_of(bands - 1)
         left = exact_dot(inverse, work[here, : (bands - 1) * w], ((1,), (0,)))
         work[here, :] = jnp.concatenate([left, inverse], axis=1)
@@ -509,7 +510,16 @@
                 target[rows, : (r + 1) * w] = piece
                 if (r + 1) * w < total:
                     target[rows, (r + 1) * w :] = jnp.zeros((w, total - (r + 1) * w), BF16)
-        gather_k.pass_on(2, 3)
+            for c in range(bands):
+                for target, piece in zip((mh, mm), split(call[r, c * w : (c + 1) * w, :], 2)):
+                    target[rows, lanes(c)] = piece
+        for start in range(0, total, WIDE):
+            wide, deep = slice(start, start + WIDE), slice(0, start + WIDE)
+            tile = split_dot(
+                [lh[wide, deep], lm[wide, deep]], [mh[deep, :], mm[deep, :]], ((1,), (0,))
+            )
+            gh[wide, :], gm[wide, :] = split(tile, 2)
+        gather_k.pass_on(3)
         gather_k.finish()
         split_blocks(kk, (kh, km))
         for copy in across_z + across_y:
@@ -526,6 +536,8 @@
             right = [lh[which, deep], lm[which, deep]]
             v = split_dot([uh[rows, deep], um[rows, deep]], right, ((1,), (1,)))
             t = split_dot([kh[rows, deep], km[rows, deep]], right, ((1,), (1,)))
+            coupled = [gh[which, :], gm[which, :]]
+            t = t - split_dot([xh[rows, :], xm[rows, :]], coupled, ((1,), (1,)))
             out = []
             for c, (j, (vw, vv)) in enumerate(zip(places, sums)):
                 vj, tj = v[:, lanes(c)], t[:, lanes(c)]
@@ -651,13 +663,14 @@
         out_specs=(VMEM, VMEM, VMEM),
         scratch_shapes=[block] * 4
         + [half] * 7
-        + [square] * 2
+        + [square] * 6
         + [
             pltpu.VMEM((total, total), F32),
             pltpu.VMEM((2, 72, w), F32),
         ]
-        + [column, column] + [chunks] * 6 + [column]
-        + [pltpu.VMEM((bands, total, w), F32), slab, slab, slab]
+        + [column, column] + [chunks] * 6
+        + [pltpu.VMEM((bands, total, w), F32)] * 2
+        + [slab, slab, slab]
         + [
             pltpu.VMEM((16, w), F32),
             pltpu.VMEM((count, 16, w), F32),
@@ -665,7 +678,8 @@
         ]
         + [dma((8, count // 2))] * 2
         + [dma((2, 3, PIECES))] * 2
-        + [dma((2, 3, count)), dma((2, 3, PIECES))]
+        + [dma((2, 3, count))] * 2
+        + [dma((2, 3, PIECES))]
         + [dma((2, PIECES))] * 2
         + [dma((count,))] * 2,
         compiler_params=pltpu.CompilerParams(

time: 204 us -> 202 us (level)
    pallas_call x1, Pallas kernels: 198 us -> 196 us  [local(): pl.pallas_call(functools.partial(iterations_kernel, count, bands, ny), ou...]
where the time goes in v5:
time: 202 us; the launch traced here: 201 us
  Pallas kernels  196 us (97%)
  local copies, waits for them, and re-layouts  4.97 us (2%)
    pallas_call x1, Pallas kernels, local(): pl.pallas_call(functools.partial(iterations_kernel, count, bands, ny), ou...  196 us

profile of v5, /device:TPU:0, one launch (start us, length us, event | category | flops | bytes accessed | tf_op | source)
XLA Modules:
  0.0 201.2 jit_solution(14109079408634773001)
XLA Ops:
  0.6 0.8 broadcast_in_dim.7
  1.5 1.0 broadcast_in_dim.8.refs_2_
  2.5 195.6 %shard_map.58 = (f32[4,256,128]{2,1,0:T(8,128)}, f32[3,128]{1,0:T(4,128)}, f32[3,128]{1,0:T(4,128)}) custom-call(f32[4,256,128]{2,1,0:T(8,128)} %bitcast.3, f32[4,256,128]{2,1,0:T(8,128)} %bitcast.4, f32[4,256,128]{2,1,0:T(8,128)} %broadcast_in_dim.8.refs_2_), custom_call_target="tpu_custom_call" | custom-call | tf_op jit(solution)/shard_map/pallas_call | solution.py:659
  198.1 0.0 copy-start.1
  198.1 1.9 copy.9
  199.9 0.0 copy-done.1
  199.9 0.0 copy-start
  200.0 0.6 copy.10
  200.5 0.1 copy-done
  200.6 0.6 copy.11
Async XLA Ops:
  198.1 1.9 copy-start.1
  199.9 0.7 copy-start
